TPU v7x, 128 devices: a whole 4x4x4 slice. The times are simulated.
128 devices in a mesh: section: 16 (over x, y_lo, core), tensor: 8 (over y_hi, z).
Axes of the slice: x: 4, y: 4 (y_hi: 2, y_lo: 2; y = y_hi * 2 + y_lo), z: 4, core: 2. Of those that a mesh axis runs over, the one named last changes fastest.
Arguments:
- arriving: bfloat16 [16, 1024, 16384], P('section', 'tensor'), may hold values from -6 to 6
- kept_input: bfloat16 [16, 1024, 16384], P('section', 'tensor'), may hold values from -6 to 6
- returning: bfloat16 [16, 1024, 16384], P('section', 'tensor'), may hold values from -6 to 6
- norm_gain: bfloat16 [16, 16384], P('section'), may hold values from 0.25 to 1.75
- key_weight: bfloat16 [16, 16384, 1024], P('section', 'tensor'), may hold values from -0.0625 to 0.0625
- value_weight: bfloat16 [16, 16384, 1024], P('section', 'tensor'), may hold values from -0.0625 to 0.0625
- key_down: bfloat16 [16, 16384, 16], P('section', 'tensor'), may hold values from -0.046875 to 0.046875
- value_down: bfloat16 [16, 16384, 16], P('section', 'tensor'), may hold values from -0.046875 to 0.046875
- key_up: bfloat16 [16, 16, 1024], P('section', None, 'tensor'), may hold values from -1.5 to 1.5
- value_up: bfloat16 [16, 16, 1024], P('section', None, 'tensor'), may hold values from -1.5 to 1.5
- key_cot: bfloat16 [16, 1024, 1024], P('section', None, 'tensor'), may hold values from -6 to 6
- value_cot: bfloat16 [16, 1024, 1024], P('section', None, 'tensor'), may hold values from -6 to 6
Outputs:
- keys: bfloat16 [16, 1024, 1024], P('section', None, 'tensor')
- values: bfloat16 [16, 1024, 1024], P('section', None, 'tensor')
- input_grad: bfloat16 [16, 1024, 16384], P('section', 'tensor')
- key_down_grad: float32 [16, 16384, 16], P('section', 'tensor')
- value_down_grad: float32 [16, 16384, 16], P('section', 'tensor')
- key_up_grad: float32 [16, 16, 1024], P('section', None, 'tensor')
- value_up_grad: float32 [16, 16, 1024], P('section', None, 'tensor')
All inputs are finite; a program needn't handle non-finite values.
Results may differ from a plain program's by a relative error of at most 0.014.
Values may be sent and summed in bfloat16 or wider, within the bound.
A program may use at most 192 MiB of HBM per device.

v0:
```python
import jax
import jax.numpy as jnp
from jax import lax
from jax.sharding import PartitionSpec as P

epsilon = 1e-05
adapter_scale = 2.0


def sent_together(arrays, axis, dim, along):
    both = jnp.concatenate(arrays, axis=along)
    out, at, finished = (lax.all_gather(both, axis, axis=dim, tiled=True), 0, [])
    for a in arrays:
        finished.append(lax.slice_in_dim(out, at, at + a.shape[along], axis=along))
        at += a.shape[along]
    return tuple(finished)


def from_behind(x, axis, by):
    count = lax.axis_size(axis)
    return lax.ppermute(x, axis, [(i, (i + by) % count) for i in range(count)])


def cut_along(x, dim, count):
    before, after = (x.shape[:dim], x.shape[dim + 1 :])
    return jnp.moveaxis(x.reshape(*before, count, -1, *after), dim, 0)


def summed_on_arrival(x, axis, dim):
    count = lax.axis_size(axis)
    tiles = lax.all_to_all(cut_along(x, dim, count), axis, 0, 0, tiled=True)
    return jnp.sum(tiles.astype(jnp.float32), axis=0)


def sent_together_2(arrays, axis, dim, along):
    widths = [a.shape[along] for a in arrays]
    both = jnp.concatenate(arrays, axis=along)
    out = summed_on_arrival(both, axis, dim)
    return tuple(jnp.split(out, [sum(widths[:k]) for k in range(1, len(widths))], axis=along))


def copy_for_each(x, axis):
    count = lax.axis_size(axis)
    return lax.all_to_all(jnp.broadcast_to(x[None], (count, *x.shape)), axis, 0, 0, tiled=True)


def of_everyone(x, axis):
    everything = copy_for_each(x, axis)
    return jnp.sum(everything, axis=0)


def packed_total(arrays, axis):
    ends = [0]
    for a in arrays:
        ends.append(ends[-1] + a.size)
    total = of_everyone(jnp.concatenate([a.ravel() for a in arrays]), axis)
    return tuple((total[b:e].reshape(a.shape) for a, b, e in zip(arrays, ends, ends[1:])))


def sent_together_3(arrays, axis, dim, along):
    ends, at = ([], 0)
    for a in arrays[:-1]:
        at += a.shape[along]
        ends.append(at)
    both = jnp.concatenate(arrays, axis=along)
    return tuple(
        jnp.split(lax.psum_scatter(both, axis, scatter_dimension=dim, tiled=True), ends, axis=along)
    )


def normalize(hidden, gain):
    values = hidden.astype(jnp.float32)
    inverse = lax.rsqrt(jnp.mean(values * values, axis=-1, keepdims=True) + epsilon)
    return (inverse, (values * inverse * gain).astype(jnp.bfloat16))


def precise_product(left, right):
    return jnp.dot(left, right, precision=lax.Precision.HIGHEST, preferred_element_type=jnp.float32)


def mixed_product(left, right):
    return jnp.dot(
        left.astype(jnp.float32), right.astype(jnp.float32), preferred_element_type=jnp.float32
    )


def token_middle(normed_input, down_whole):
    key_middle = mixed_product(normed_input, down_whole[0])
    value_middle = mixed_product(normed_input, down_whole[1])
    return sent_together((key_middle, value_middle), "tensor", 0, 1)


def on_device(
    arriving,
    kept_input,
    returning,
    norm_gain,
    key_weight,
    value_weight,
    key_down,
    value_down,
    key_up,
    value_up,
    key_cot,
    value_cot,
):
    gain = norm_gain[0].astype(jnp.float32)
    incoming = from_behind(arriving, "section", 1)[0]
    back = from_behind(returning, "section", -1)[0]
    kept = kept_input[0]
    key_matrix = key_weight[0]
    value_matrix = value_weight[0]
    key_down_matrix = key_down[0]
    value_down_matrix = value_down[0]
    key_up_matrix = key_up[0]
    value_up_matrix = value_up[0]
    key_cotangent = key_cot[0]
    value_cotangent = value_cot[0]
    tok_rows = incoming.shape[0]
    _, normed_input = normalize(incoming, gain)
    spread = lax.all_to_all(normed_input, "tensor", split_axis=1, concat_axis=0, tiled=True)
    key_partial = mixed_product(spread, key_matrix)
    value_partial = mixed_product(spread, value_matrix)
    down_whole = sent_together((key_down_matrix, value_down_matrix), "tensor", 0, 1)
    fwd_mids = token_middle(normed_input, down_whole)
    key_sum, value_sum = sent_together_2(
        (key_partial.astype(jnp.bfloat16), value_partial.astype(jnp.bfloat16)), "tensor", 1, 0
    )
    key_sum = key_sum + adapter_scale * precise_product(
        fwd_mids[0], key_up_matrix.astype(jnp.float32)
    )
    value_sum = value_sum + adapter_scale * precise_product(
        fwd_mids[1], value_up_matrix.astype(jnp.float32)
    )
    keys = key_sum.astype(jnp.bfloat16)[None]
    values = value_sum.astype(jnp.bfloat16)[None]
    adapted_key, adapted_value = packed_total(
        (
            mixed_product(key_cotangent, key_up_matrix.T),
            mixed_product(value_cotangent, value_up_matrix.T),
        ),
        "tensor",
    )
    pieces = sent_together((key_cotangent, value_cotangent), "tensor", 1, 0)
    total = mixed_product(pieces[0], key_matrix.T)
    branch_output = total + mixed_product(pieces[1], value_matrix.T)
    branch_output = branch_output + adapter_scale * (
        precise_product(adapted_key, key_down_matrix.T.astype(jnp.float32))
        + precise_product(adapted_value, value_down_matrix.T.astype(jnp.float32))
    )
    branch_rows = lax.all_to_all(
        branch_output.astype(jnp.bfloat16), "tensor", split_axis=0, concat_axis=1, tiled=True
    )
    inverse, kept_normed = normalize(kept, gain)
    kept_values = kept.astype(jnp.float32)
    scaled = gain * branch_rows.astype(jnp.float32)
    inner = jnp.mean(kept_values * scaled, axis=-1, keepdims=True)
    input_grad = (
        back.astype(jnp.float32)
        + inverse * scaled
        - kept_values * inverse * inverse * inverse * inner
    ).astype(jnp.bfloat16)
    backward_middles = token_middle(kept_normed, down_whole)
    offset = lax.axis_index("tensor") * tok_rows
    mine_key = lax.dynamic_slice_in_dim(adapted_key, offset, tok_rows, 0)
    mine_value = lax.dynamic_slice_in_dim(adapted_value, offset, tok_rows, 0)
    saved_wide_input = kept_normed.astype(jnp.float32)
    key_down_gradient, value_down_gradient = tuple(
        (
            part.astype(jnp.float32)
            for part in sent_together_3(
                (
                    (adapter_scale * precise_product(saved_wide_input.T, mine_key)).astype(
                        jnp.bfloat16
                    ),
                    (adapter_scale * precise_product(saved_wide_input.T, mine_value)).astype(
                        jnp.bfloat16
                    ),
                ),
                "tensor",
                0,
                1,
            )
        )
    )
    key_up_gradient = adapter_scale * precise_product(
        backward_middles[0].T, key_cotangent.astype(jnp.float32)
    )
    value_up_gradient = adapter_scale * precise_product(
        backward_middles[1].T, value_cotangent.astype(jnp.float32)
    )
    return (
        keys,
        values,
        input_grad[None],
        key_down_gradient[None],
        value_down_gradient[None],
        key_up_gradient[None],
        value_up_gradient[None],
    )


def solution(mesh):
    return jax.shard_map(
        on_device,
        mesh=mesh,
        in_specs=(
            P("section", "tensor", None),
            P("section", "tensor", None),
            P("section", "tensor", None),
            P("section", None),
            P("section", "tensor", None),
            P("section", "tensor", None),
            P("section", "tensor", None),
            P("section", "tensor", None),
            P("section", None, "tensor"),
            P("section", None, "tensor"),
            P("section", None, "tensor"),
            P("section", None, "tensor"),
        ),
        out_specs=(
            P("section", None, "tensor"),
            P("section", None, "tensor"),
            P("section", "tensor", None),
            P("section", "tensor", None),
            P("section", "tensor", None),
            P("section", None, "tensor"),
            P("section", None, "tensor"),
        ),
        check_vma=False,
    )
```

profile of v0, /device:TPU:1, one launch (start us, length us, event | category | flops | bytes accessed | tf_op | source)
XLA Modules:
  0.0 476.0 jit_solution(3411973312623718253)
XLA Ops:
  7.2 0.0 copy-start
  7.2 0.0 all-gather.5.cloned.1.call-start
  7.2 1.9 pad_maximum_fusion.1
  9.1 0.0 all-gather.5.cloned.1.call-update
  9.2 6.4 %copy.54 = bf16[1,128,16384]{1,2,0:T(8,128)(2,1)} copy(bf16[1,128,16384]{2,1,0:T(8,128)(2,1)} %param.12) | data formatting | bytes 8388608 | tf_op args[0]
  15.6 2.7 collective-permute-start
  18.4 0.2 fusion.64
  18.6 0.2 reshape.182
  18.8 0.2 fusion.61
  19.0 0.2 reshape.183
  19.2 1.5 broadcast_in_dim.39
  20.7 7.4 %all-to-all-start.2 = ((f32[8,1,32768]{2,1,0:T(1,128)}), f32[8,1,32768]{2,1,0:T(1,128)S(1)}, u32[]{:S(2)}, u32[]{:S(2)}) async-start(f32[8,1,32768]{2,1,0:T(1,128)} %broadcast_in_dim.39), calls=%async_computation.2 | async-start | bytes 2097152 | tf_op jit(solution)/shard_map/all_to_all | solution.py:44
  28.1 0.0 all-gather.3.cloned.1.call-start
  28.2 0.7 pad_maximum_fusion.2
  28.8 0.0 all-gather.3.cloned.1.call-update
  28.9 0.2 convert_reduce_fusion.1
  29.1 56.9 %all-to-all-done.2 = f32[8,1,32768]{2,1,0:T(1,128)S(1)} async-done(((f32[8,1,32768]{2,1,0:T(1,128)}), f32[8,1,32768]{2,1,0:T(1,128)S(1)}, u32[]{:S(2)}, u32[]{:S(2)}) %all-to-all-start.2) | async-done | bytes 1048608 | tf_op jit(solution)/shard_map/all_to_all | solution.py:44
  86.0 0.8 reduce_sum.48
  86.8 3.8 fusion.16
  90.6 5.8 %multiply_convert_fusion = bf16[128,8,2048]{0,2,1:T(8,128)(2,1)} fusion(f32[8,2048]{1,0:T(8,128)S(1)} %mul.145, f32[128]{0:T(128)S(1)} %add_rsqrt_fusion.1, bf16[128,8,2048]{0,2,1:T(8,128)(2,1)} %bitcast.110), kind=kLoop, calls=%fused_computation.30 | loop fusion | flops 8388608 | bytes 8454656 | tf_op jit(solution)/shard_map/convert_element_type | solution.py:74
  96.4 4.8 %all-to-all-start = ((bf16[128,8,2048]{0,2,1:T(8,128)(2,1)}), bf16[128,8,2048]{0,2,1:T(8,128)(2,1)}, u32[]{:S(2)}, u32[]{:S(2)}) async-start(bf16[128,8,2048]{0,2,1:T(8,128)(2,1)} %multiply_convert_fusion), calls=%async_computation | async-start | bytes 8388608 | tf_op jit(solution)/shard_map/all_to_all | solution.py:121
  101.2 0.2 slice.57
  101.4 0.2 slice.59
  101.6 5.6 %fusion.74 = f32[1024,2048]{1,0:T(8,128)} fusion(f32[1024,16]{1,0:T(8,128)S(1)} %slice.57, bf16[1,2048,16]{1,2,0:T(8,128)(2,1)S(1)} %copy-done.10), kind=kOutput, calls=%fused_computation.97 | convolution fusion | flops 402653184 | bytes 8519680 | tf_op jit(solution)/shard_map/dot_general | solution.py:78
  107.2 53.0 %all-gather.5.cloned.1.call-done = bf16[2048,1024]{1,0:T(8,128)(2,1)} async-done(((bf16[2048,128]{1,0:T(8,128)(2,1)}), bf16[2048,1024]{1,0:T(8,128)(2,1)}) %all-gather.5.cloned.1.call-update) | async-done | bytes 4194320 | tf_op jit(solution)/shard_map/all_gather | solution.py:12
  160.1 7.1 %fusion.19 = f32[1024,2048]{1,0:T(8,128)S(1)} fusion(bf16[1,2048,1024]{2,1,0:T(8,128)(2,1)} %param.17, bf16[2048,1024]{1,0:T(8,128)(2,1)} %all-gather.5.cloned.1.call-done), kind=kOutput, calls=%fused_computation.33 | convolution fusion | flops 4294967296 | bytes 14680064 | tf_op jit(solution)/shard_map/dot_general | solution.py:82
  167.3 6.7 %fusion.23 = f32[1024,2048]{1,0:T(8,128)} fusion(bf16[1,2048,1024]{2,1,0:T(8,128)(2,1)S(1)} %copy-done.15, bf16[2048,1024]{1,0:T(8,128)(2,1)S(1)} %copy-done.17), kind=kOutput, calls=%fused_computation.37 | convolution fusion | flops 4294967296 | bytes 14680064 | tf_op jit(solution)/shard_map/dot_general | solution.py:82
  174.1 8.9 %add_convert_fusion = bf16[1024,2048]{1,0:T(8,128)(2,1)} fusion(f32[1024,2048]{1,0:T(8,128)S(1)} %bitcast.121, f32[1024,2048]{1,0:T(8,128)} %fusion.23, f32[1024,2048]{1,0:T(8,128)S(1)} %fusion.19, f32[1024,16]{1,0:T(8,128)S(1)} %slice.59, bf16[1,2048,16]{1,2,0:T(8,128)(2,1)} %param.19), kind=kOutput, calls=%fused_computation.28 | convolution fusion | flops 413138944 | bytes 29491200 | tf_op jit(solution)/shard_map/dot_general | solution.py:78
  182.9 4.6 all-to-all-start.3
  187.5 6.4 %copy.57 = bf16[1,128,16384]{1,2,0:T(8,128)(2,1)} copy(bf16[1,128,16384]{2,1,0:T(8,128)(2,1)} %param.14) | data formatting | bytes 8388608 | tf_op args[2]
  193.9 0.5 collective-permute-start.1
  194.5 0.1 convert_element_type.122
  194.6 6.4 %copy.58 = bf16[1,128,16384]{1,2,0:T(8,128)(2,1)} copy(bf16[1,128,16384]{2,1,0:T(8,128)(2,1)} %param.13) | data formatting | bytes 8388608 | tf_op args[1]
  201.0 79.2 %all-gather.3.cloned.1.call-done = bf16[16384,32]{0,1:T(8,128)(2,1)} async-done(((bf16[2048,32]{0,1:T(8,128)(2,1)}), bf16[16384,32]{0,1:T(8,128)(2,1)}) %all-gather.3.cloned.1.call-update) | async-done | bytes 1048592 | tf_op jit(solution)/shard_map/all_gather | solution.py:12
  280.1 8.6 %fusion.39 = f32[128,16]{0,1:T(8,128)S(1)} fusion(bf16[1,128,16384]{1,2,0:T(8,128)(2,1)} %collective-permute-done, f32[16384]{0:T(1024)S(1)} %bitcast.127, f32[128]{0:T(128)S(1)} %add_rsqrt_fusion.1, bf16[16384,32]{0,1:T(8,128)(2,1)} %all-gather.3.cloned.1.call-done), kind=kOutput, calls=%fused_computation.51 | convolution fusion | flops 75497472 | bytes 4792832 | tf_op jit(solution)/shard_map/dot_general | solution.py:82
  288.7 4.7 fusion.41
  293.4 27.8 %all_gather.13 = f32[1024,32]{0,1:T(8,128)S(1)} all-gather(f32[128,32]{0,1:T(8,128)S(1)} %pad_maximum_fusion.4), channel_id=1, replica_groups=mesh['section'=16,'tensor'=8] {'tensor'}, dimensions={0}, use_global_device_ids=true | all-gather | bytes 147456 | tf_op jit(solution)/shard_map/all_gather | solution.py:12
  321.3 6.4 %copy.55 = bf16[8,128,2048]{2,1,0:T(8,128)(2,1)} copy(bf16[8,128,2048]{1,2,0:T(8,128)(2,1)} %bitcast.2) | data formatting | bytes 8388608 | tf_op jit(solution)/shard_map/all_to_all | solution.py:121
  327.7 8.1 %fusion.29 = bf16[1024,1024]{1,0:T(8,128)(2,1)S(1)} fusion(bf16[1024,2048]{1,0:T(8,128)(2,1)} %bitcast.123, bf16[1,2048,1024]{2,1,0:T(8,128)(2,1)} %param.16), kind=kOutput, calls=%fused_computation.43 | convolution fusion | flops 4296015872 | bytes 10485760 | tf_op jit(solution)/shard_map/dot_general | solution.py:82
  335.8 4.7 fusion.32
  340.5 2.4 bitcast_bitcast_fusion
  342.9 4.6 all-to-all-start.1
  347.5 0.3 reduce-scatter.2.cloned.1.call-start
  347.9 6.5 %convert_bitcast_fusion.1 = f32[128,8,2048]{2,0,1:T(8,128)} fusion(bf16[8,128,2048]{2,1,0:T(8,128)(2,1)} %all-to-all-done.3), kind=kLoop, calls=%fused_computation.27 | loop fusion | flops 2097152 | bytes 12582912 | tf_op jit(solution)/shard_map/convert_element_type | solution.py:156
  354.3 9.1 %copy.62 = f32[128,8,2048]{0,2,1:T(8,128)} copy(f32[128,8,2048]{2,0,1:T(8,128)} %convert_bitcast_fusion.1) | data formatting | bytes 16777216 | tf_op jit(solution)/shard_map/convert_element_type | solution.py:156
  363.5 6.5 %fusion.5 = (f32[128]{0:T(128)S(1)}, f32[128]{0:T(128)S(1)}) fusion(bf16[1,128,16384]{1,2,0:T(8,128)(2,1)} %copy.58, f32[128,8,2048]{0,2,1:T(8,128)} %copy.62, f32[16384]{0:T(1024)S(1)} %bitcast.129), kind=kLoop, calls=%fused_computation.9 | loop fusion | flops 12582656 | bytes 12649472 | tf_op jit(solution)/shard_map/reduce_sum | solution.py:73
  370.0 6.9 %fusion.8 = bf16[128,16384]{0,1:T(8,128)(2,1)S(1)} fusion(bf16[1,128,16384]{1,2,0:T(8,128)(2,1)S(1)} %copy-done.3, f32[128]{0:T(128)S(1)} %add_rsqrt_fusion, f32[16384]{0:T(1024)S(1)} %bitcast.130), kind=kLoop, calls=%fused_computation.12 | loop fusion | flops 8388608 | bytes 8454656 | tf_op jit(solution)/shard_map/convert_element_type | solution.py:74
  377.0 3.5 fusion
  380.4 3.5 fusion.1
  383.9 1.1 pad_maximum_fusion
  385.0 0.0 reduce-scatter.2.cloned.1.call-update
  385.1 9.1 %fusion.13 = bf16[1,128,16384]{1,2,0:T(8,128)(2,1)} fusion(bf16[1,128,16384]{1,2,0:T(8,128)(2,1)} %copy.58, f32[128,8,2048]{0,2,1:T(8,128)} %copy.62, bf16[1,128,16384]{1,2,0:T(8,128)(2,1)} %collective-permute-done.1, f32[128]{0:T(128)S(1)} %broadcast_multiply_fusion, f32[16384]{0:T(1024)S(1)} %bitcast.131, f32[128]{0:T(128)S(1)} %add_rsqrt_fusion), kind=kLoop, calls=%fused_computation.17 | loop fusion | flops 23068672 | bytes 21038080 | tf_op jit(solution)/shard_map/convert_element_type | solution.py:162
  394.1 6.4 %copy.64 = bf16[1,128,16384]{2,1,0:T(8,128)(2,1)} copy(bf16[1,128,16384]{1,2,0:T(8,128)(2,1)} %fusion.13) | data formatting | bytes 8388608
  400.5 3.0 fusion.48
  403.5 0.4 copy-done.2
  403.9 0.7 fusion.51
  404.6 28.3 %all_gather.15 = f32[1024,32]{0,1:T(8,128)S(1)} all-gather(f32[128,32]{0,1:T(8,128)S(1)} %pad_maximum_fusion.5), channel_id=1, replica_groups=mesh['section'=16,'tensor'=8] {'tensor'}, dimensions={0}, use_global_device_ids=true | all-gather | bytes 147456 | tf_op jit(solution)/shard_map/all_gather | solution.py:12
  432.9 0.8 fusion.45
  433.7 0.8 fusion.46
  434.5 2.9 convert_reduce_fusion
  437.5 1.3 fusion.44
  438.8 1.3 fusion.43
  440.1 27.8 %reduce-scatter.2.cloned.1.call-done = bf16[2048,32]{0,1:T(8,128)(2,1)} async-done(((bf16[16384,32]{0,1:T(8,128)(2,1)}), bf16[2048,32]{0,1:T(8,128)(2,1)}) %reduce-scatter.2.cloned.1.call-update) | async-done | bytes 131088 | tf_op jit(solution)/shard_map/reduce_scatter | solution.py:67
  467.9 1.6 fusion.55
  (52 shorter events, 0.2 us)
Async XLA Ops:
  7.2 11.6 %copy-start = (bf16[1,16,128]{2,1,0:T(8,128)(2,1)S(1)}, bf16[1,16,128]{2,1,0:T(8,128)(2,1)}, u32[]{:S(2)}) copy-start(bf16[1,16,128]{2,1,0:T(8,128)(2,1)} %param.21) | copy-start | bytes 12292
  7.2 152.9 %all-gather.5.cloned.1.call-start = ((), (), s32[]{:S(2)}) async-start(), calls=%async_computation.6 | async-start | bytes 4718592 | tf_op jit(solution)/shard_map/all_gather | solution.py:12
  9.2 9.2 %copy-start.7 = (bf16[1,1024,128]{2,1,0:T(8,128)(2,1)S(1)}, bf16[1,1024,128]{2,1,0:T(8,128)(2,1)}, u32[]{:S(2)}) copy-start(bf16[1,1024,128]{2,1,0:T(8,128)(2,1)} %param.22) | copy-start | bytes 786436
  9.2 9.2 %copy-start.14 = (bf16[1,16,128]{2,1,0:T(8,128)(2,1)S(1)}, bf16[1,16,128]{2,1,0:T(8,128)(2,1)}, u32[]{:S(2)}) copy-start(bf16[1,16,128]{2,1,0:T(8,128)(2,1)} %param.20) | copy-start | bytes 12292
  9.2 9.6 %copy-start.5 = (bf16[1,1024,128]{2,1,0:T(8,128)(2,1)S(1)}, bf16[1,1024,128]{2,1,0:T(8,128)(2,1)}, u32[]{:S(2)}) copy-start(bf16[1,1024,128]{2,1,0:T(8,128)(2,1)} %param.23) | copy-start | bytes 786436
  15.6 12.5 %copy-start.10 = (bf16[1,2048,16]{1,2,0:T(8,128)(2,1)S(1)}, bf16[1,2048,16]{1,2,0:T(8,128)(2,1)}, u32[]{:S(2)}) copy-start(bf16[1,2048,16]{1,2,0:T(8,128)(2,1)} %param.18) | copy-start | bytes 196612
  15.6 12.5 %copy-start.11 = (bf16[1,2048,16]{1,2,0:T(8,128)(2,1)S(1)}, bf16[1,2048,16]{1,2,0:T(8,128)(2,1)}, u32[]{:S(2)}) copy-start(bf16[1,2048,16]{1,2,0:T(8,128)(2,1)} %param.19) | copy-start | bytes 196612
  15.6 13.2 %copy-start.12 = (bf16[1,16384]{1,0:T(2,128)(2,1)S(1)}, bf16[1,16384]{1,0:T(2,128)(2,1)}, u32[]{:S(2)}) copy-start(bf16[1,16384]{1,0:T(2,128)(2,1)} %param.15) | copy-start | bytes 98308
  15.6 71.2 %collective-permute-start = (bf16[1,128,16384]{1,2,0:T(8,128)(2,1)}, bf16[1,128,16384]{1,2,0:T(8,128)(2,1)}, u32[]{:S(2)}, u32[]{:S(2)}) collective-permute-start(bf16[1,128,16384]{1,2,0:T(8,128)(2,1)} %copy.54), channel_id=1, source_target_pairs={{0,8},{8,16},{16,24},{24,32},{32,40},{40,48},{48,56},{56,64},{64,7... | collective-permute-start | bytes 12582920 | tf_op jit(solution)/shard_map/ppermute | solution.py:21
  20.7 65.3 %all-to-all-start.2 = ((f32[8,1,32768]{2,1,0:T(1,128)}), f32[8,1,32768]{2,1,0:T(1,128)S(1)}, u32[]{:S(2)}, u32[]{:S(2)}) async-start(f32[8,1,32768]{2,1,0:T(1,128)} %broadcast_in_dim.39), calls=%async_computation.2 | async-start | bytes 2097152 | tf_op jit(solution)/shard_map/all_to_all | solution.py:44
  28.1 252.0 %all-gather.3.cloned.1.call-start = ((), (), s32[]{:S(2)}) async-start(), calls=%async_computation.5 | async-start | bytes 1179648 | tf_op jit(solution)/shard_map/all_gather | solution.py:12
  96.4 86.5 %all-to-all-start = ((bf16[128,8,2048]{0,2,1:T(8,128)(2,1)}), bf16[128,8,2048]{0,2,1:T(8,128)(2,1)}, u32[]{:S(2)}, u32[]{:S(2)}) async-start(bf16[128,8,2048]{0,2,1:T(8,128)(2,1)} %multiply_convert_fusion), calls=%async_computation | async-start | bytes 8388608 | tf_op jit(solution)/shard_map/all_to_all | solution.py:121
  160.1 7.2 %copy-start.15 = (bf16[1,2048,1024]{2,1,0:T(8,128)(2,1)S(1)}, bf16[1,2048,1024]{2,1,0:T(8,128)(2,1)}, u32[]{:S(2)}) copy-start(bf16[1,2048,1024]{2,1,0:T(8,128)(2,1)} %param.16) | copy-start | bytes 12582916
  160.1 7.2 %copy-start.17 = (bf16[2048,1024]{1,0:T(8,128)(2,1)S(1)}, bf16[2048,1024]{1,0:T(8,128)(2,1)}, u32[]{:S(2)}) copy-start(bf16[2048,1024]{1,0:T(8,128)(2,1)} %all-gather.5.cloned.1.call-done) | copy-start | bytes 12582916
  160.1 13.9 %slice-start = ((s8[8388608]{0:T(1024)(128)(4,1)}), s8[4194304]{0:T(1024)(128)(4,1)S(1)}, s32[]{:S(2)}) async-start(s8[8388608]{0:T(1024)(128)(4,1)} %bitcast.120), calls=%async_computation.8 | async-start | bytes 8388608
  167.3 6.8 %slice-start.1 = ((s8[8388608]{0:T(1024)(128)(4,1)}), s8[4194304]{0:T(1024)(128)(4,1)S(1)}, s32[]{:S(2)}) async-start(s8[8388608]{0:T(1024)(128)(4,1)} %bitcast.120), calls=%async_computation.9 | async-start | bytes 8388608
  182.9 160.0 %all-to-all-start.3 = ((bf16[8,128,2048]{2,1,0:T(8,128)(2,1)}), bf16[8,128,2048]{2,1,0:T(8,128)(2,1)}, u32[]{:S(2)}, u32[]{:S(2)}) async-start(bf16[8,128,2048]{2,1,0:T(8,128)(2,1)} %bitcast.122), calls=%async_computation.3 | async-start | bytes 8388608 | tf_op jit(solution)/shard_map/all_to_all | solution.py:151
  187.5 7.0 %copy-start.13 = (bf16[1,16384]{1,0:T(2,128)(2,1)S(1)}, bf16[1,16384]{1,0:T(2,128)(2,1)}, u32[]{:S(2)}) copy-start(bf16[1,16384]{1,0:T(2,128)(2,1)} %param.15) | copy-start | bytes 98308
  193.9 191.1 %collective-permute-start.1 = (bf16[1,128,16384]{1,2,0:T(8,128)(2,1)}, bf16[1,128,16384]{1,2,0:T(8,128)(2,1)}, u32[]{:S(2)}, u32[]{:S(2)}) collective-permute-start(bf16[1,128,16384]{1,2,0:T(8,128)(2,1)} %copy.57), channel_id=1, source_target_pairs={{0,120},{8,0},{16,8},{24,16},{32,24},{40,32},{48,40},{56,48},{64,5... | collective-permute-start | bytes 12582920 | tf_op jit(solution)/shard_map/ppermute | solution.py:21
  280.1 8.6 %copy-start.9 = (bf16[16384,32]{0,1:T(8,128)(2,1)S(1)}, bf16[16384,32]{0,1:T(8,128)(2,1)}, u32[]{:S(2)}) copy-start(bf16[16384,32]{0,1:T(8,128)(2,1)} %all-gather.3.cloned.1.call-done) | copy-start | bytes 3145732
  327.7 8.1 %copy-start.4 = (bf16[8,128,2048]{2,1,0:T(8,128)(2,1)S(1)}, bf16[8,128,2048]{2,1,0:T(8,128)(2,1)}, u32[]{:S(2)}) copy-start(bf16[8,128,2048]{2,1,0:T(8,128)(2,1)} %copy.55) | copy-start | bytes 12582916
  327.7 8.1 %copy-start.16 = (bf16[1,2048,1024]{2,1,0:T(8,128)(2,1)S(1)}, bf16[1,2048,1024]{2,1,0:T(8,128)(2,1)}, u32[]{:S(2)}) copy-start(bf16[1,2048,1024]{2,1,0:T(8,128)(2,1)} %param.17) | copy-start | bytes 12582916
  342.9 91.6 %all-to-all-start.1 = ((bf16[8,2048,128]{2,1,0:T(8,128)(2,1)}), bf16[8,2048,128]{2,1,0:T(8,128)(2,1)}, u32[]{:S(2)}, u32[]{:S(2)}) async-start(bf16[8,2048,128]{2,1,0:T(8,128)(2,1)} %bitcast_bitcast_fusion), calls=%async_computation.1 | async-start | bytes 8388608 | tf_op jit(solution)/shard_map/all_to_all | solution.py:31
  347.5 120.4 %reduce-scatter.2.cloned.1.call-start = ((), (), s32[]{:S(2)}) async-start(), calls=%async_computation.7 | async-start | bytes 1179648 | tf_op jit(solution)/shard_map/reduce_scatter | solution.py:67
  363.5 6.5 %copy-start.3 = (bf16[1,128,16384]{1,2,0:T(8,128)(2,1)S(1)}, bf16[1,128,16384]{1,2,0:T(8,128)(2,1)}, u32[]{:S(2)}) copy-start(bf16[1,128,16384]{1,2,0:T(8,128)(2,1)} %copy.58) | copy-start | bytes 12582916
  377.0 7.0 %copy-start.1 = (bf16[128,16384]{0,1:T(8,128)(2,1)}, bf16[128,16384]{0,1:T(8,128)(2,1)S(1)}, u32[]{:S(2)}) copy-start(bf16[128,16384]{0,1:T(8,128)(2,1)S(1)} %fusion.8) | copy-start | bytes 12582916
  400.5 3.4 copy-start.2
  400.5 32.4 %copy-start.6 = (bf16[1,1024,128]{2,1,0:T(8,128)(2,1)S(1)}, bf16[1,1024,128]{2,1,0:T(8,128)(2,1)}, u32[]{:S(2)}) copy-start(bf16[1,1024,128]{2,1,0:T(8,128)(2,1)} %param.23) | copy-start | bytes 786436
  400.5 33.2 %copy-start.8 = (bf16[1,1024,128]{2,1,0:T(8,128)(2,1)S(1)}, bf16[1,1024,128]{2,1,0:T(8,128)(2,1)}, u32[]{:S(2)}) copy-start(bf16[1,1024,128]{2,1,0:T(8,128)(2,1)} %param.22) | copy-start | bytes 786436
Sparse Core Ops, SparseCore 0:
  10.2 149.8 all-gather.4
  163.0 117.1 all-gather.2
  385.2 82.7 reduce-scatter.1
where the time goes:
time: 479 us; the launch traced here: 476 us
  waiting for transfers between devices  217 us (45%)
  matrix products  69.7 us (15%)
  blocking collectives  56.1 us (12%)
  other arithmetic  50.2 us (10%)
  local copies, waits for them, and re-layouts  44 us (9%)
  starting transfers between devices  25 us (5%)
  between operations  14.1 us (3%)
    all_gather x2, waiting for transfers between devices, sent_together(): lax.all_gather(both, axis, axis=dim, tiled=True)  132 us
    all_to_all x1, waiting for transfers between devices, copy_for_each(): lax.all_to_all(jnp.broadcast_to(x[None], (count, *x.shape)), axis, 0, 0,...  56.9 us
    all_gather x2, blocking collectives, sent_together(): lax.all_gather(both, axis, axis=dim, tiled=True)  56.1 us
    dot_general x10, matrix products, mixed_product(): jnp.dot(left.astype(jnp.float32), right.astype(jnp.float32), preferred_el...  44 us
    reduce_scatter x1, waiting for transfers between devices, sent_together_3(): lax.psum_scatter(both, axis, scatter_dimension=dim, tiled=True)  27.8 us
    unnamed x44, local copies, waits for them, and re-layouts  26.1 us
    dot_general x8, matrix products, precise_product(): jnp.dot(left, right, precision=lax.Precision.HIGHEST, preferred_element_t...  25.6 us
    convert_element_type x2, other arithmetic, normalize(): return (inverse, (values * inverse * gain).astype(jnp.bfloat16))  12.7 us
  transfers between devices with their start and end apart: 9, of which 4 were waited for; matrix products, arithmetic and copies ran while one was open for 34% of the time, Pallas kernels for 0%

commit v1 on v0

v1 whole, which is shorter than its diff:
```python
import functools

import jax
import jax.numpy as jnp
from jax import lax
from jax.experimental import pallas as pl
from jax.experimental.pallas import tpu as pltpu
from jax.sharding import PartitionSpec as P

EPS = 1e-05
SCALE = 2.0
F32 = jnp.float32
BF16 = jnp.bfloat16
MESH = pl.DeviceIdType.MESH

UPK, UPV, DNK, DNV, COTK, COTV, XIN, INV, RET, BRA, GRD, MID = range(12)
KINDS = 12


def dot(a, b, ca, cb):
    return lax.dot_general(a, b, (((ca,), (cb,)), ((), ())), preferred_element_type=F32)


def kernel(
    S, T, G,
    arr, kept, ret, gain, wk, wv, dkt, dvt, uk, uv, ck, cv,
    keys, vals, igrad, gkt, gvt, guk, guv,
    wb, cf, xin, kb, back, bro, bri, yo, yi, dnf, gdo, gdi, upf, inv_o, inv_i, mid_o, mid_i, inv_b,
    ss, rs, yss, yrs, ls, ols,
):
    sec = lax.axis_index("section")
    t = lax.axis_index("tensor")
    R = arr.shape[0]
    DS = wk.shape[0]
    H = ck.shape[1]
    KV = wk.shape[1]
    RK = uk.shape[0]
    D = T * DS
    nxt = lax.rem(sec + 1, S)
    prv = lax.rem(sec + S - 1, S)

    def to(i):
        return lax.rem(t + i, T)

    def frm(i):
        return lax.rem(t + T - i, T)

    def blk(i, size):
        return pl.ds(pl.multiple_of(i * size, size), size)

    def send(src, dst, kind, i, device):
        return pltpu.make_async_remote_copy(
            src_ref=src, dst_ref=dst, send_sem=ss.at[kind, i], recv_sem=rs.at[kind, i],
            device_id=device, device_id_type=MESH,
        )

    bar = pltpu.get_barrier_semaphore()
    for i in range(1, T):
        pl.semaphore_signal(bar, inc=1, device_id=(sec, to(i)), device_id_type=MESH)
    for i in range(T):
        pl.semaphore_signal(bar, inc=1, device_id=(nxt, to(i)), device_id_type=MESH)
        pl.semaphore_signal(bar, inc=1, device_id=(prv, to(i)), device_id_type=MESH)
    pl.semaphore_wait(bar, 3 * T - 1)

    def small(i):
        dev = (sec, to(i))
        return (
            send(uk, upf.at[pl.ds(0, RK), blk(t, H)], UPK, i, dev),
            send(uv, upf.at[pl.ds(RK, RK), pl.ds(pl.multiple_of(KV + t * H, H), H)], UPV, i, dev),
            send(dkt, dnf.at[pl.ds(0, RK), blk(t, DS)], DNK, i, dev),
            send(dvt, dnf.at[pl.ds(RK, RK), blk(t, DS)], DNV, i, dev),
        )

    def cots(i):
        dev = (sec, to(i))
        return (
            send(ck, cf.at[:, blk(t, H)], COTK, i, dev),
            send(cv, cf.at[:, pl.ds(pl.multiple_of(KV + t * H, H), H)], COTV, i, dev),
        )

    def xs(i):
        return send(arr.at[:, blk(to(i), DS)], xin.at[blk(t, R), :], XIN, i, (nxt, to(i)))

    def invs(i):
        return send(inv_o, inv_i.at[i], INV, i, (nxt, to(i)))

    def rets():
        return send(ret, back, RET, 0, (prv, t))

    def bras(i):
        return send(bro.at[to(i)], bri.at[i], BRA, i, (sec, to(i)))

    def grds(i):
        return send(gdo.at[to(i)], gdi.at[i], GRD, i, (sec, to(i)))

    def mids(i):
        return send(mid_o, mid_i.at[i], MID, i, (sec, to(i)))

    RG = R * T // G

    def ysend(g, i):
        p = to(i)
        out = []
        for v in range(2):
            out.append(pltpu.make_async_remote_copy(
                src_ref=yo.at[pl.ds(g * RG, RG), pl.ds(pl.multiple_of(v * KV + p * H, H), H)],
                dst_ref=yi.at[i, pl.ds(g * RG, RG), pl.ds(v * H, H)],
                send_sem=yss.at[2 * g + v, i], recv_sem=yrs.at[2 * g + v, i],
                device_id=(sec, p), device_id_type=MESH,
            ))
        return out

    for i in range(1, T):
        for c in small(i):
            c.start()
    for i in range(1, T):
        for c in cots(i):
            c.start()
    for i in range(T):
        xs(i).start()
    rets().start()

    loc = [
        pltpu.make_async_copy(wk, wb.at[:, pl.ds(0, KV)], ls.at[0]),
        pltpu.make_async_copy(wv, wb.at[:, pl.ds(KV, KV)], ls.at[1]),
        pltpu.make_async_copy(uk, upf.at[pl.ds(0, RK), blk(t, H)], ls.at[2]),
        pltpu.make_async_copy(uv, upf.at[pl.ds(RK, RK), pl.ds(pl.multiple_of(KV + t * H, H), H)], ls.at[3]),
        pltpu.make_async_copy(dkt, dnf.at[pl.ds(0, RK), blk(t, DS)], ls.at[4]),
        pltpu.make_async_copy(dvt, dnf.at[pl.ds(RK, RK), blk(t, DS)], ls.at[5]),
        pltpu.make_async_copy(ck, cf.at[:, blk(t, H)], ls.at[6]),
        pltpu.make_async_copy(cv, cf.at[:, pl.ds(pl.multiple_of(KV + t * H, H), H)], ls.at[7]),
        pltpu.make_async_copy(kept, kb, ls.at[8]),
    ]
    arrs = [pltpu.make_async_copy(arr.at[:, pl.ds(j * DS, DS)], bro.at[j], ls.at[9 + j]) for j in range(T)]
    for c in arrs:
        c.start()
    for c in loc:
        c.start()
    upf[pl.ds(0, RK), pl.ds(KV, KV)] = jnp.zeros((RK, KV), BF16)
    upf[pl.ds(RK, RK), pl.ds(0, KV)] = jnp.zeros((RK, KV), BF16)

    for c in arrs:
        c.wait()

    def sq_a(j, acc):
        v = bro[j].astype(F32)
        return acc + jnp.sum(v * v, axis=-1, keepdims=True)

    total = lax.fori_loop(0, T, sq_a, jnp.zeros((R, 1), F32))
    inverse = lax.rsqrt(total / D + EPS)
    inv_o[...] = jnp.broadcast_to(inverse, (R, R)).T[0:8, :]
    for i in range(T):
        invs(i).start()

    for c in loc:
        c.wait()

    def sq_b(j, acc):
        v = kb[:, blk(j, DS)].astype(F32)
        return acc + jnp.sum(v * v, axis=-1, keepdims=True)

    total = lax.fori_loop(0, T, sq_b, jnp.zeros((R, 1), F32))
    inv_b[...] = jnp.broadcast_to(lax.rsqrt(total / D + EPS), (R, R))

    def wait_small(i):
        dev = (sec, to(i))
        r = frm(i)
        send(uk, upf.at[pl.ds(0, RK), blk(r, H)], UPK, i, dev).wait_recv()
        send(uv, upf.at[pl.ds(RK, RK), pl.ds(pl.multiple_of(KV + r * H, H), H)], UPV, i, dev).wait_recv()
        send(dkt, dnf.at[pl.ds(0, RK), blk(r, DS)], DNK, i, dev).wait_recv()
        send(dvt, dnf.at[pl.ds(RK, RK), blk(r, DS)], DNV, i, dev).wait_recv()

    for i in range(1, T):
        wait_small(i)
    WT = 256

    def weff(j, _):
        down = dnf[:, pl.ds(pl.multiple_of(t * DS + j * WT, WT), WT)]
        low = dot(down, upf[...], 0, 0)
        rows = blk(j, WT)
        wb[rows, :] = (wb[rows, :].astype(F32) + SCALE * low).astype(BF16)
        return 0

    lax.fori_loop(0, DS // WT, weff, 0)

    for i in range(1, T):
        r = frm(i)
        dev = (sec, to(i))
        send(ck, cf.at[:, blk(r, H)], COTK, i, dev).wait_recv()
        send(cv, cf.at[:, pl.ds(pl.multiple_of(KV + r * H, H), H)], COTV, i, dev).wait_recv()
    NT = 512

    def branch(p, store):
        c = cf[blk(p, R), :]
        for n in range(DS // NT):
            store(n, dot(c, wb[pl.ds(n * NT, NT), :], 1, 1).astype(BF16))

    def branch_to(i, _):
        p = to(i)

        def store(n, v):
            bro[p, :, pl.ds(n * NT, NT)] = v

        branch(p, store)
        bras(i).start()
        return 0

    lax.fori_loop(1, T, branch_to, 0)

    def store_own(n, v):
        bri[0, :, pl.ds(n * NT, NT)] = v

    branch(t, store_own)

    adapt = (SCALE * dot(upf[...], cf[blk(t, R), :], 1, 1)).astype(BF16)

    def kept_block(i, mid):
        p = to(i)
        cols = blk(p, DS)
        normed = (kb[:, cols].astype(F32) * inv_b[:, 0:1] * gain[:, cols].astype(F32)).astype(BF16)
        gdo[p] = dot(adapt, normed, 1, 0).astype(BF16)

        @pl.when(i > 0)
        def _():
            grds(i).start()

        return mid + dot(dnf[:, cols], normed, 1, 1)

    mid = lax.fori_loop(0, T, kept_block, jnp.zeros((2 * RK, R), F32))
    mid_o[...] = mid.astype(BF16)
    for i in range(1, T):
        mids(i).start()

    def forward(i, _):
        r = frm(i)
        send(arr.at[:, blk(to(i), DS)], xin.at[blk(r, R), :], XIN, i, (nxt, to(i))).wait_recv()
        invs(i).wait_recv()
        inv = jnp.broadcast_to(inv_i[i, 0:1, :], (R, R)).T
        normed = (
            xin[blk(r, R), :].astype(F32) * inv[:, 0:1] * gain[:, blk(t, DS)].astype(F32)
        ).astype(BF16)
        rows = blk(i, R)
        for n in range(2 * KV // NT):
            yo[rows, pl.ds(n * NT, NT)] = dot(normed, wb[:, pl.ds(n * NT, NT)], 1, 0).astype(BF16)
        return 0

    for g in range(G):
        lax.fori_loop(g * (T // G), (g + 1) * (T // G), forward, 0)
        for i in range(1, T):
            for c in ysend(g, i):
                c.start()

    for i in range(1, T):
        grds(i).wait_recv()
        mids(i).wait_recv()
    g = gdo[t].astype(F32)
    for i in range(1, T):
        g = g + gdi[i].astype(F32)
    gkt[...] = g[0:RK]
    gvt[...] = g[RK : 2 * RK]

    def up_grad(i, acc):
        r = frm(i)
        m = mid_i[i]
        rows = blk(r, R)
        k = dot(m[0:RK], cf[rows, blk(t, H)], 1, 0)
        v = dot(m[RK : 2 * RK], cf[rows, pl.ds(pl.multiple_of(KV + t * H, H), H)], 1, 0)
        return acc[0] + k, acc[1] + v

    mid_i[0] = mid_o[...]
    k, v = lax.fori_loop(0, T, up_grad, (jnp.zeros((RK, H), F32), jnp.zeros((RK, H), F32)))
    guk[...] = SCALE * k
    guv[...] = SCALE * v

    for i in range(1, T):
        bras(i).wait_recv()

    def inner_block(i, acc):
        cols = blk(frm(i), DS)
        scaled = gain[:, cols].astype(F32) * bri[i].astype(F32)
        return acc + jnp.sum(kb[:, cols].astype(F32) * scaled, axis=-1, keepdims=True)

    inner = lax.fori_loop(0, T, inner_block, jnp.zeros((R, 1), F32)) / D
    send(ret, back, RET, 0, (prv, t)).wait_recv()
    inverse = inv_b[:, 0:1]
    factor = inverse * inverse * inverse * inner

    def final_block(i, _):
        cols = blk(frm(i), DS)
        scaled = gain[:, cols].astype(F32) * bri[i].astype(F32)
        back[:, cols] = (
            back[:, cols].astype(F32) + inverse * scaled - kb[:, cols].astype(F32) * factor
        ).astype(BF16)
        pltpu.make_async_copy(back.at[:, cols], igrad.at[:, cols], ols.at[i]).start()
        return 0

    lax.fori_loop(0, T, final_block, 0)

    for g in range(G):
        for i in range(1, T):
            for c in ysend(g, i):
                c.wait_recv()

    def total_block(b, _):
        own = blk(lax.rem(t + T - b, T), R)
        k = yo[own, blk(t, H)].astype(F32)
        v = yo[own, pl.ds(pl.multiple_of(KV + t * H, H), H)].astype(F32)
        for i in range(1, T):
            rows = blk(lax.rem(t + 2 * T - i - b, T), R)
            k = k + yi[i, rows, pl.ds(0, H)].astype(F32)
            v = v + yi[i, rows, pl.ds(H, H)].astype(F32)
        keys[blk(b, R), :] = k.astype(BF16)
        vals[blk(b, R), :] = v.astype(BF16)
        return 0

    lax.fori_loop(0, T, total_block, 0)

    for i in range(1, T):
        for c in (*small(i), *cots(i), bras(i), grds(i), mids(i)):
            c.wait_send()
        for g in range(G):
            for c in ysend(g, i):
                c.wait_send()
    for i in range(T):
        xs(i).wait_send()
        invs(i).wait_send()
        cols = blk(frm(i), DS)
        pltpu.make_async_copy(back.at[:, cols], igrad.at[:, cols], ols.at[i]).wait()
    rets().wait_send()


def on_device(S, T, arr, kept, ret, gain, wk, wv, dk, dv, uk, uv, ck, cv):
    G = 2
    _, R, D = arr.shape
    _, DS, KV = wk.shape
    RK, H = uk.shape[1:]
    any_ = pl.BlockSpec(memory_space=pl.ANY)
    vmem = pl.BlockSpec(memory_space=pltpu.VMEM)
    outs = pl.pallas_call(
        functools.partial(kernel, S, T, G),
        out_shape=(
            jax.ShapeDtypeStruct((R * T, H), BF16),
            jax.ShapeDtypeStruct((R * T, H), BF16),
            jax.ShapeDtypeStruct((R, D), BF16),
            jax.ShapeDtypeStruct((RK, DS), F32),
            jax.ShapeDtypeStruct((RK, DS), F32),
            jax.ShapeDtypeStruct((RK, H), F32),
            jax.ShapeDtypeStruct((RK, H), F32),
        ),
        in_specs=[any_, any_, any_, vmem] + [any_] * 8,
        out_specs=(vmem, vmem, any_, vmem, vmem, vmem, vmem),
        scratch_shapes=[
            pltpu.VMEM((DS, 2 * KV), BF16),
            pltpu.VMEM((R * T, 2 * KV), BF16),
            pltpu.VMEM((R * T, DS), BF16),
            pltpu.VMEM((R, D), BF16),
            pltpu.VMEM((R, D), BF16),
            pltpu.VMEM((T, R, DS), BF16),
            pltpu.VMEM((T, R, DS), BF16),
            pltpu.VMEM((R * T, 2 * KV), BF16),
            pltpu.VMEM((T, R * T, 2 * H), BF16),
            pltpu.VMEM((2 * RK, D), BF16),
            pltpu.VMEM((T, 2 * RK, DS), BF16),
            pltpu.VMEM((T, 2 * RK, DS), BF16),
            pltpu.VMEM((2 * RK, 2 * KV), BF16),
            pltpu.VMEM((8, R), F32),
            pltpu.VMEM((T, 8, R), F32),
            pltpu.VMEM((2 * RK, R), BF16),
            pltpu.VMEM((T, 2 * RK, R), BF16),
            pltpu.VMEM((R, R), F32),
            pltpu.SemaphoreType.DMA((KINDS, T)),
            pltpu.SemaphoreType.DMA((KINDS, T)),
            pltpu.SemaphoreType.DMA((2 * G, T)),
            pltpu.SemaphoreType.DMA((2 * G, T)),
            pltpu.SemaphoreType.DMA((9 + T,)),
            pltpu.SemaphoreType.DMA((T,)),
        ],
        compiler_params=pltpu.CompilerParams(
            collective_id=0, has_side_effects=True, vmem_limit_bytes=62 * 2**20
        ),
    )(
        arr[0], kept[0], ret[0], gain, wk[0], wv[0], dk[0].T, dv[0].T, uk[0], uv[0], ck[0], cv[0]
    )
    keys, vals, igrad, gkt, gvt, guk, guv = outs
    return keys[None], vals[None], igrad[None], gkt.T[None], gvt.T[None], guk[None], guv[None]


def solution(mesh):
    S, T = mesh.shape["section"], mesh.shape["tensor"]
    return jax.shard_map(
        functools.partial(on_device, S, T),
        mesh=mesh,
        in_specs=(
            P("section", "tensor", None),
            P("section", "tensor", None),
            P("section", "tensor", None),
            P("section", None),
            P("section", "tensor", None),
            P("section", "tensor", None),
            P("section", "tensor", None),
            P("section", "tensor", None),
            P("section", None, "tensor"),
            P("section", None, "tensor"),
            P("section", None, "tensor"),
            P("section", None, "tensor"),
        ),
        out_specs=(
            P("section", None, "tensor"),
            P("section", None, "tensor"),
            P("section", "tensor", None),
            P("section", "tensor", None),
            P("section", "tensor", None),
            P("section", None, "tensor"),
            P("section", None, "tensor"),
        ),
        check_vma=False,
    )
```

time: 479 us -> 325 us (0.68)
  the two profiles are of different devices: /device:TPU:1 before, /device:TPU:104 now
where the time goes in v1:
time: 325 us
  Pallas kernels  314 us (97%)
  local copies, waits for them, and re-layouts  10.5 us (3%)
    pallas_call x1, Pallas kernels, on_device(): pl.pallas_call(functools.partial(kernel, S, T, G), out_shape=(jax.ShapeDt...  314 us
    unnamed x15, local copies, waits for them, and re-layouts  10.5 us

profile of v1, /device:TPU:104, one launch (start us, length us, event | category | flops | bytes accessed | tf_op | source)
XLA Modules:
  0.0 324.8 jit_solution(11750619156666102566)
XLA Ops:
  0.6 313.7 %shard_map.171 = (bf16[1024,128]{1,0:T(8,128)(2,1)}, bf16[1024,128]{1,0:T(8,128)(2,1)}, bf16[128,16384]{1,0:T(8,128)(2,1)}, f32[16,2048]{1,0:T(8,128)}, f32[16,2...) custom-call(bf16[128,16384]{1,0:T(8,128)(2,1)} %bitcast.26, bf16[128,16384]{1,0:T(8,128)(2,1)} %bitcast.27, ...), custom_call_target="tpu_custom_call" | custom-call | tf_op jit(solution)/shard_map/pallas_call | solution.py:339
  314.3 1.7 copy.26
  316.0 1.7 copy.27
  317.6 0.0 copy-start.1
  317.6 0.0 copy-start
  317.6 0.0 copy-start.3
  317.6 0.0 copy-start.2
  317.6 4.6 %copy.28 = bf16[1,128,16384]{2,1,0:T(8,128)(2,1)} copy(bf16[1,128,16384]{2,1,0:T(8,128)(2,1)} %bitcast.31) | data formatting | bytes 8388608
  322.3 0.0 copy-done.1
  322.3 0.7 copy.29
  322.9 0.0 copy-done
  322.9 0.7 copy.30
  323.6 0.0 copy-done.3
  323.6 0.6 copy.31
  324.2 0.0 copy-done.2
  324.2 0.6 copy.32
Async XLA Ops:
  317.6 4.6 %copy-start.1 = (f32[16,2048]{1,0:T(8,128)S(1)}, f32[16,2048]{1,0:T(8,128)}, u32[]{:S(2)}) copy-start(f32[16,2048]{1,0:T(8,128)} %get-tuple-element.17) | copy-start | bytes 393220
  317.6 5.3 %copy-start = (f32[16,2048]{1,0:T(8,128)S(1)}, f32[16,2048]{1,0:T(8,128)}, u32[]{:S(2)}) copy-start(f32[16,2048]{1,0:T(8,128)} %get-tuple-element.18) | copy-start | bytes 393220
  317.6 5.9 %copy-start.3 = (f32[16,128]{1,0:T(8,128)S(1)}, f32[16,128]{1,0:T(8,128)}, u32[]{:S(2)}) copy-start(f32[16,128]{1,0:T(8,128)} %get-tuple-element.19) | copy-start | bytes 24580
  317.6 6.5 %copy-start.2 = (f32[16,128]{1,0:T(8,128)S(1)}, f32[16,128]{1,0:T(8,128)}, u32[]{:S(2)}) copy-start(f32[16,128]{1,0:T(8,128)} %get-tuple-element.20) | copy-start | bytes 24580

commit v2 on v1

v2 whole, which is shorter than its diff:
```python
import contextlib
import functools

import jax
import jax.numpy as jnp
from jax import lax
from jax.experimental import pallas as pl
from jax.experimental.pallas import tpu as pltpu
from jax.sharding import PartitionSpec as P

EPS = 1e-05
SCALE = 2.0
F32 = jnp.float32
BF16 = jnp.bfloat16
MESH = pl.DeviceIdType.MESH

UPK, UPV, DNK, DNV, COT, XAT, XIN, INV, RET, BRA, GRD, MID, PAR, TOT = range(14)
KINDS = 14


PROFILE = False


def scope(name):
    return jax.named_scope(name) if PROFILE else contextlib.nullcontext()


def dot(a, b, ca, cb):
    return lax.dot_general(a, b, (((ca,), (cb,)), ((), ())), preferred_element_type=F32)


def kernel(
    S, Y, Z,
    arr, kept, ret, gain, wk, wv, dkt, dvt, uk, uv, ck, cv,
    keys, vals, igrad, gkt, gvt, guk, guv,
    wb, cf, xin, xat, kb, back, bro, bri, yo, yi, yco, yci, yt, ys, yr, dnf, gdo, gdi, upf,
    inv_o, inv_i, mid_o, mid_i, inv_b,
    ss, rs, css, crs, yss, yrs, ls, ols,
):
    sec = lax.axis_index("section")
    t = lax.axis_index("tensor")
    T = Y * Z
    R = arr.shape[0]
    DS = wk.shape[0]
    H = ck.shape[1]
    KV = wk.shape[1]
    RK = uk.shape[0]
    D = T * DS
    nxt = lax.rem(sec + 1, S)
    prv = lax.rem(sec + S - 1, S)
    y = t // Z
    z = lax.rem(t, Z)

    def to(i):
        return lax.rem(y + i // Z, Y) * Z + lax.rem(z + lax.rem(i, Z), Z)

    def frm(i):
        return lax.rem(y + Y - i // Z, Y) * Z + lax.rem(z + Z - lax.rem(i, Z), Z)

    def blk(i, size):
        return pl.ds(pl.multiple_of(i * size, size), size)

    def vblk(i):
        return pl.ds(pl.multiple_of(KV + i * H, H), H)

    def remote(src, dst, ssem, rsem, device):
        return pltpu.make_async_remote_copy(
            src_ref=src, dst_ref=dst, send_sem=ssem, recv_sem=rsem,
            device_id=device, device_id_type=MESH,
        )

    def send(src, dst, kind, i, device):
        return remote(src, dst, ss.at[kind, i], rs.at[kind, i], device)

    def ups(i, r):
        dev = (sec, to(i))
        return (
            send(uk, upf.at[pl.ds(0, RK), blk(r, H)], UPK, i, dev),
            send(uv, upf.at[pl.ds(RK, RK), vblk(r)], UPV, i, dev),
        )

    def downs(i, r):
        dev = (sec, to(i))
        return (
            send(dkt, dnf.at[pl.ds(0, RK), blk(r, DS)], DNK, i, dev),
            send(dvt, dnf.at[pl.ds(RK, RK), blk(r, DS)], DNV, i, dev),
        )

    def cot_part(v, i, q, r, own):
        at, to_at = (blk(q, H), blk(r, H)) if v == 0 else (vblk(q), vblk(r))
        dy, dz = i // Z, i % Z
        if dz == 2:
            dev = (sec, to(1 if v == 0 else Z - 1))
        else:
            dev = (sec, to(dz if dz else dy * Z))
        src = (ck, cv)[v] if own else cf.at[:, at]
        return remote(src, cf.at[:, to_at], css.at[v, i], crs.at[v, i], dev)

    def cots(i, q, r, own=False):
        return [cot_part(v, i, q, r, own) for v in range(2)]

    def xfirst(i, r):
        dy, dz = i // Z, i % Z
        cols = blk(lax.rem(y + dy, Y) * Z + lax.rem(z + dz, Z), DS)
        dst = xin.at[blk(r, R), :] if dz == 0 else xat.at[dy * (Z - 1) + dz - 1]
        return send(arr.at[:, cols], dst, XAT, i, (nxt, to(dy * Z)))

    def xon(i, q, r):
        dy, dz = i // Z, i % Z
        return send(xat.at[dy * (Z - 1) + dz - 1], xin.at[blk(r, R), :], XIN, i, (sec, to(dz)))

    def invs(i):
        return send(inv_o, inv_i.at[i], INV, i, (nxt, to(i)))

    def rets():
        return send(ret, back, RET, 0, (prv, t))

    def bras(i):
        return send(bro.at[to(i)], bri.at[i], BRA, i, (sec, to(i)))

    def grds(i):
        return send(gdo.at[to(i)], gdi.at[i], GRD, i, (sec, to(i)))

    def mids(i):
        return send(mid_o, mid_i.at[i], MID, i, (sec, to(i)))

    RG = R * Z

    def parts(g, k):
        v = k % 2
        dz = (1, Z - 1, Z - 1, 1)[k]
        zz = lax.rem(z + (2 if k < 2 else dz), Z)
        out = []
        for w in range(Y):
            at = pl.multiple_of(v * KV + (w * Z + zz) * H, H)
            n = (g * 4 + k) * Y + w
            out.append(remote(
                yo.at[pl.ds(g * RG, RG), pl.ds(at, H)],
                yi.at[k, pl.ds(g * RG, RG), pl.ds(w * H, H)],
                yss.at[n], yrs.at[n], (sec, to(dz)),
            ))
        return out

    def pairs(g, v, row):
        return send(yco.at[v, blk(row, RG), :], yci.at[v, blk(row, RG), :], PAR, g * 2 + v, (sec, to(1 if v == 0 else Z - 1)))

    def tots(g, dy, row):
        return send(ys.at[dy, blk(row, RG), :], yr.at[dy, blk(row, RG), :], TOT, g * Y + dy, (sec, to(dy * Z)))

    bar = pltpu.get_barrier_semaphore()
    for i in range(1, T):
        pl.semaphore_signal(bar, inc=1, device_id=(sec, to(i)), device_id_type=MESH)
    for i in range(T):
        pl.semaphore_signal(bar, inc=1, device_id=(nxt, to(i)), device_id_type=MESH)
        pl.semaphore_signal(bar, inc=1, device_id=(prv, to(i)), device_id_type=MESH)

    arrs = [pltpu.make_async_copy(arr.at[:, pl.ds(j * DS, DS)], bro.at[j], ls.at[9 + j]) for j in range(T)]
    loc = [
        pltpu.make_async_copy(wk, wb.at[:, pl.ds(0, KV)], ls.at[0]),
        pltpu.make_async_copy(wv, wb.at[:, pl.ds(KV, KV)], ls.at[1]),
        pltpu.make_async_copy(uk, upf.at[pl.ds(0, RK), blk(t, H)], ls.at[2]),
        pltpu.make_async_copy(uv, upf.at[pl.ds(RK, RK), vblk(t)], ls.at[3]),
        pltpu.make_async_copy(dkt, dnf.at[pl.ds(0, RK), blk(t, DS)], ls.at[4]),
        pltpu.make_async_copy(dvt, dnf.at[pl.ds(RK, RK), blk(t, DS)], ls.at[5]),
        pltpu.make_async_copy(ck, cf.at[:, blk(t, H)], ls.at[6]),
        pltpu.make_async_copy(cv, cf.at[:, vblk(t)], ls.at[7]),
        pltpu.make_async_copy(kept, kb, ls.at[8]),
    ]
    for c in arrs:
        c.start()
    for c in loc:
        c.start()
    upf[pl.ds(0, RK), pl.ds(KV, KV)] = jnp.zeros((RK, KV), BF16)
    upf[pl.ds(RK, RK), pl.ds(0, KV)] = jnp.zeros((RK, KV), BF16)

    with scope("barrier"):
        pl.semaphore_wait(bar, 3 * T - 1)

    for i in range(1, T):
        for c in ups(i, t):
            c.start()
    for dy in range(1, Y):
        for c in cots(dy * Z, t, t, True):
            c.start()
    for i in (1, Z - 1):
        for c in cots(i, t, t, True):
            c.start()
    with scope("stats_a"):
        for c in arrs:
            c.wait()

        def sq_a(j, acc):
            v = bro[j].astype(F32)
            return acc + jnp.sum(v * v, axis=-1, keepdims=True)

        total = lax.fori_loop(0, T, sq_a, jnp.zeros((R, 1), F32))
        inverse = lax.rsqrt(total / D + EPS)
        inv_o[...] = jnp.broadcast_to(inverse, (R, R)).T[0:8, :]
        for i in range(T):
            invs(i).start()

    def cot_wait(i):
        for c in cots(i, t, frm(i)):
            c.wait_recv()

    def cot_halves(dy):
        for v in range(2):
            q = frm(dy * Z + (1 if v == 0 else Z - 1))
            cot_part(v, dy * Z + 2, q, q, False).start()

    with scope("cot_on"):
        for dy in range(1, Y):
            cot_wait(dy * Z)
            q = frm(dy * Z)
            for dz in (1, Z - 1):
                for c in cots(dy * Z + dz, q, q):
                    c.start()
        for i in (1, Z - 1):
            cot_wait(i)
        cot_halves(0)
        for i in range(T):
            xfirst(i, t).start()

    with scope("stats_b"):
        for c in loc:
            c.wait()

        def sq_b(j, acc):
            v = kb[:, blk(j, DS)].astype(F32)
            return acc + jnp.sum(v * v, axis=-1, keepdims=True)

        total = lax.fori_loop(0, T, sq_b, jnp.zeros((R, 1), F32))
        inv_b[...] = jnp.broadcast_to(lax.rsqrt(total / D + EPS), (R, R))

    with scope("weff"):
        for i in range(1, T):
            for c in ups(i, frm(i)):
                c.wait_recv()
        WT = 256

        def weff(j, _):
            down = dnf[:, pl.ds(pl.multiple_of(t * DS + j * WT, WT), WT)]
            low = dot(down, upf[...], 0, 0)
            rows = blk(j, WT)
            wb[rows, :] = (wb[rows, :].astype(F32) + SCALE * low).astype(BF16)
            return 0

        lax.fori_loop(0, DS // WT, weff, 0)

    def x_on(dy):
        with scope("x_on"):
            for dz in range(1, Z):
                i = dy * Z + dz
                xfirst(i, frm(dy * Z)).wait_recv()
                xon(i, 0, frm(dy * Z)).start()

    with scope("wait_cot"):
        for dy in range(1, Y):
            for dz in (1, Z - 1):
                cot_wait(dy * Z + dz)
            cot_halves(dy)
        for dy in range(Y):
            cot_wait(dy * Z + 2)
    for i in range(1, T):
        for c in downs(i, t):
            c.start()
    for dy in range(Y):
        x_on(dy)
    rets().start()
    NT = 512

    def branch(p, store):
        c = cf[blk(p, R), :]
        for n in range(DS // NT):
            store(n, dot(c, wb[pl.ds(n * NT, NT), :], 1, 1).astype(BF16))

    def branch_to(i, _):
        p = to(i)

        def store(n, v):
            bro[p, :, pl.ds(n * NT, NT)] = v

        branch(p, store)
        return 0

    def store_own(n, v):
        bri[0, :, pl.ds(n * NT, NT)] = v

    with scope("branch"):
        lax.fori_loop(1, T, branch_to, 0)
        branch(t, store_own)

    def forward_block(i, r):
        invs(i).wait_recv()
        inv = jnp.broadcast_to(inv_i[i, 0:1, :], (R, R)).T
        normed = (
            xin[blk(r, R), :].astype(F32) * inv[:, 0:1] * gain[:, blk(t, DS)].astype(F32)
        ).astype(BF16)
        rows = blk(i, R)
        for n in range(2 * KV // NT):
            yo[rows, pl.ds(n * NT, NT)] = dot(normed, wb[:, pl.ds(n * NT, NT)], 1, 0).astype(BF16)

    def forward(i, _):
        forward_block(i, frm(i))
        return 0

    with scope("wait_x"):
        for i in range(T):
            if i % Z:
                send(xat.at[0], xin.at[blk(frm(i), R), :], XIN, i, (sec, to(i % Z))).wait_recv()
    for i in range(1, T):
        bras(i).start()

    with scope("forward"):
        for g in range(Y):
            xfirst(g * Z, frm(g * Z)).wait_recv()
            forward_block(g * Z, frm(g * Z))
            lax.fori_loop(g * Z + 1, (g + 1) * Z, forward, 0)
            for k in range(4):
                for c in parts(g, k):
                    c.start()

    with scope("kept"):
        for i in range(1, T):
            for c in downs(i, frm(i)):
                c.wait_recv()
        adapt = (SCALE * dot(upf[...], cf[blk(t, R), :], 1, 1)).astype(BF16)

        def kept_block(i, mid):
            p = to(i)
            cols = blk(p, DS)
            normed = (kb[:, cols].astype(F32) * inv_b[:, 0:1] * gain[:, cols].astype(F32)).astype(BF16)
            gdo[p] = dot(adapt, normed, 1, 0).astype(BF16)

            @pl.when(i > 0)
            def _():
                grds(i).start()

            return mid + dot(dnf[:, cols], normed, 1, 1)

        mid = lax.fori_loop(0, T, kept_block, jnp.zeros((2 * RK, R), F32))
        mid_o[...] = mid.astype(BF16)
        for i in range(1, T):
            mids(i).start()

    def rows_of(g, b, j):
        return blk(g * Z + lax.rem(z + 2 * Z - j - b, Z), R)

    def heads(v, hy, zz):
        return pl.ds(pl.multiple_of(v * KV + (hy * Z + zz) * H, H), H)

    for g in range(Y):
        with scope("wait_relay"):
            for k in range(2):
                for c in parts(g, k):
                    c.wait_recv()
        row = lax.rem(y + Y - g, Y)

        with scope("relay"):

            def pair_block(b, _):
                dst = blk(row * Z + b, R)
                for v in range(2):
                    zz = lax.rem(z + (1 if v == 0 else Z - 1), Z)
                    for w in range(Y):
                        acc = yo[rows_of(g, b, 0), heads(v, w, zz)].astype(F32)
                        acc = acc + yi[v, rows_of(g, b, 1 if v == 0 else Z - 1), pl.ds(w * H, H)].astype(F32)
                        yco[v, dst, pl.ds(w * H, H)] = acc.astype(BF16)
                return 0

            lax.fori_loop(0, Z, pair_block, 0)
            for v in range(2):
                pairs(g, v, row).start()

    with scope("wait_branch"):
        for i in range(1, T):
            bras(i).wait_recv()

    with scope("inner"):

        def inner_block(i, acc):
            cols = blk(frm(i), DS)
            scaled = gain[:, cols].astype(F32) * bri[i].astype(F32)
            return acc + jnp.sum(kb[:, cols].astype(F32) * scaled, axis=-1, keepdims=True)

        inner = lax.fori_loop(0, T, inner_block, jnp.zeros((R, 1), F32)) / D
    with scope("wait_ret"):
        rets().wait_recv()
    with scope("final"):
        inverse = inv_b[:, 0:1]
        factor = inverse * inverse * inverse * inner

        def final_block(i, _):
            cols = blk(frm(i), DS)
            scaled = gain[:, cols].astype(F32) * bri[i].astype(F32)
            back[:, cols] = (
                back[:, cols].astype(F32) + inverse * scaled - kb[:, cols].astype(F32) * factor
            ).astype(BF16)
            pltpu.make_async_copy(back.at[:, cols], igrad.at[:, cols], ols.at[i]).start()
            return 0

        lax.fori_loop(0, T, final_block, 0)

    for g in range(Y):
        with scope("wait_parts"):
            for k in (2, 3):
                for c in parts(g, k):
                    c.wait_recv()
            for v in range(2):
                pairs(g, v, lax.rem(y + Y - g, Y)).wait_recv()
        row = lax.rem(y + Y - g, Y)

        with scope("sum_parts"):

            def sum_block(b, _):
                dst = blk(row * Z + b, R)
                for w in range(Y):
                    hy = lax.rem(y + w, Y)
                    for v in range(2):
                        acc = yo[rows_of(g, b, 0), heads(v, hy, z)].astype(F32)
                        acc = acc + yi[2 + v, rows_of(g, b, Z - 1 if v == 0 else 1), blk(hy, H)].astype(F32)
                        acc = acc + yci[v, dst, blk(hy, H)].astype(F32)
                        if w == 0:
                            yt[dst, pl.ds(v * H, H)] = acc
                        else:
                            ys[w, dst, pl.ds(v * H, H)] = acc.astype(BF16)
                return 0

            lax.fori_loop(0, Z, sum_block, 0)
            for dy in range(1, Y):
                tots(g, dy, row).start()

    with scope("grads"):
        for i in range(1, T):
            grds(i).wait_recv()
            mids(i).wait_recv()
        g = gdo[t].astype(F32)
        for i in range(1, T):
            g = g + gdi[i].astype(F32)
        gkt[...] = g[0:RK]
        gvt[...] = g[RK : 2 * RK]

        def up_grad(i, acc):
            m = mid_i[i]
            rows = blk(frm(i), R)
            k = dot(m[0:RK], cf[rows, blk(t, H)], 1, 0)
            v = dot(m[RK : 2 * RK], cf[rows, vblk(t)], 1, 0)
            return acc[0] + k, acc[1] + v

        mid_i[0] = mid_o[...]
        k, v = lax.fori_loop(0, T, up_grad, (jnp.zeros((RK, H), F32), jnp.zeros((RK, H), F32)))
        guk[...] = SCALE * k
        guv[...] = SCALE * v

    with scope("wait_tot"):
        for g in range(Y):
            for dy in range(1, Y):
                tots(g, dy, lax.rem(y + 2 * Y - dy - g, Y)).wait_recv()

    def total_block(b, _):
        rows = blk(b, R)
        k = yt[rows, pl.ds(0, H)]
        v = yt[rows, pl.ds(H, H)]
        for dy in range(1, Y):
            k = k + yr[dy, rows, pl.ds(0, H)].astype(F32)
            v = v + yr[dy, rows, pl.ds(H, H)].astype(F32)
        keys[rows, :] = k.astype(BF16)
        vals[rows, :] = v.astype(BF16)
        return 0

    with scope("total"):
        lax.fori_loop(0, T, total_block, 0)

    with scope("end"):
        for i in range(1, T):
            for c in (*ups(i, t), *downs(i, t), bras(i), grds(i), mids(i)):
                c.wait_send()
        for i in range(1, T):
            for c in cots(i, t, t):
                c.wait_send()
        for g in range(Y):
            for k in range(4):
                for c in parts(g, k):
                    c.wait_send()
            for v in range(2):
                pairs(g, v, lax.rem(y + Y - g, Y)).wait_send()
            for dy in range(1, Y):
                tots(g, dy, lax.rem(y + Y - g, Y)).wait_send()
        for i in range(T):
            xfirst(i, t).wait_send()
            if i % Z:
                xon(i, 0, t).wait_send()
            invs(i).wait_send()
            cols = blk(frm(i), DS)
            pltpu.make_async_copy(back.at[:, cols], igrad.at[:, cols], ols.at[i]).wait()
        rets().wait_send()


def on_device(S, T, arr, kept, ret, gain, wk, wv, dk, dv, uk, uv, ck, cv):
    Y, Z = 2, T // 2
    _, R, D = arr.shape
    _, DS, KV = wk.shape
    RK, H = uk.shape[1:]
    any_ = pl.BlockSpec(memory_space=pl.ANY)
    vmem = pl.BlockSpec(memory_space=pltpu.VMEM)
    outs = pl.pallas_call(
        functools.partial(kernel, S, Y, Z),
        out_shape=(
            jax.ShapeDtypeStruct((R * T, H), BF16),
            jax.ShapeDtypeStruct((R * T, H), BF16),
            jax.ShapeDtypeStruct((R, D), BF16),
            jax.ShapeDtypeStruct((RK, DS), F32),
            jax.ShapeDtypeStruct((RK, DS), F32),
            jax.ShapeDtypeStruct((RK, H), F32),
            jax.ShapeDtypeStruct((RK, H), F32),
        ),
        in_specs=[any_, any_, any_, vmem] + [any_] * 8,
        out_specs=(vmem, vmem, any_, vmem, vmem, vmem, vmem),
        scratch_shapes=[
            pltpu.VMEM((DS, 2 * KV), BF16),
            pltpu.VMEM((R * T, 2 * KV), BF16),
            pltpu.VMEM((R * T, DS), BF16),
            pltpu.VMEM((Y * (Z - 1), R, DS), BF16),
            pltpu.VMEM((R, D), BF16),
            pltpu.VMEM((R, D), BF16),
            pltpu.VMEM((T, R, DS), BF16),
            pltpu.VMEM((T, R, DS), BF16),
            pltpu.VMEM((R * T, 2 * KV), BF16),
            pltpu.VMEM((4, R * T, Y * H), BF16),
            pltpu.VMEM((2, R * T, Y * H), BF16),
            pltpu.VMEM((2, R * T, Y * H), BF16),
            pltpu.VMEM((R * T, 2 * H), F32),
            pltpu.VMEM((Y, R * T, 2 * H), BF16),
            pltpu.VMEM((Y, R * T, 2 * H), BF16),
            pltpu.VMEM((2 * RK, D), BF16),
            pltpu.VMEM((T, 2 * RK, DS), BF16),
            pltpu.VMEM((T, 2 * RK, DS), BF16),
            pltpu.VMEM((2 * RK, 2 * KV), BF16),
            pltpu.VMEM((8, R), F32),
            pltpu.VMEM((T, 8, R), F32),
            pltpu.VMEM((2 * RK, R), BF16),
            pltpu.VMEM((T, 2 * RK, R), BF16),
            pltpu.VMEM((R, R), F32),
            pltpu.SemaphoreType.DMA((KINDS, T)),
            pltpu.SemaphoreType.DMA((KINDS, T)),
            pltpu.SemaphoreType.DMA((2, T)),
            pltpu.SemaphoreType.DMA((2, T)),
            pltpu.SemaphoreType.DMA((4 * Y * Y,)),
            pltpu.SemaphoreType.DMA((4 * Y * Y,)),
            pltpu.SemaphoreType.DMA((9 + T,)),
            pltpu.SemaphoreType.DMA((T,)),
        ],
        compiler_params=pltpu.CompilerParams(
            collective_id=0, has_side_effects=True, vmem_limit_bytes=62 * 2**20
        ),
    )(
        arr[0], kept[0], ret[0], gain, wk[0], wv[0], dk[0].T, dv[0].T, uk[0], uv[0], ck[0], cv[0]
    )
    keys, vals, igrad, gkt, gvt, guk, guv = outs
    return keys[None], vals[None], igrad[None], gkt.T[None], gvt.T[None], guk[None], guv[None]


def solution(mesh):
    S, T = mesh.shape["section"], mesh.shape["tensor"]
    return jax.shard_map(
        functools.partial(on_device, S, T),
        mesh=mesh,
        in_specs=(
            P("section", "tensor", None),
            P("section", "tensor", None),
            P("section", "tensor", None),
            P("section", None),
            P("section", "tensor", None),
            P("section", "tensor", None),
            P("section", "tensor", None),
            P("section", "tensor", None),
            P("section", None, "tensor"),
            P("section", None, "tensor"),
            P("section", None, "tensor"),
            P("section", None, "tensor"),
        ),
        out_specs=(
            P("section", None, "tensor"),
            P("section", None, "tensor"),
            P("section", "tensor", None),
            P("section", "tensor", None),
            P("section", "tensor", None),
            P("section", None, "tensor"),
            P("section", None, "tensor"),
        ),
        check_vma=False,
    )
```

time: 325 us -> 225 us (0.69)
  the two profiles are of different devices: /device:TPU:104 before, /device:TPU:1 now
where the time goes in v2:
time: 225 us
  Pallas kernels  214 us (95%)
  local copies, waits for them, and re-layouts  10.5 us (5%)
    pallas_call x1, Pallas kernels, on_device(): pl.pallas_call(functools.partial(kernel, S, Y, Z), out_shape=(jax.ShapeDt...  214 us
    unnamed x15, local copies, waits for them, and re-layouts  10.5 us

profile of v2, /device:TPU:1, one launch (start us, length us, event | category | flops | bytes accessed | tf_op | source)
XLA Modules:
  0.0 225.2 jit_solution(17312590098611452403)
XLA Ops:
  0.6 214.0 %shard_map.171 = (bf16[1024,128]{1,0:T(8,128)(2,1)}, bf16[1024,128]{1,0:T(8,128)(2,1)}, bf16[128,16384]{1,0:T(8,128)(2,1)}, f32[16,2048]{1,0:T(8,128)}, f32[16,2...) custom-call(bf16[128,16384]{1,0:T(8,128)(2,1)} %bitcast.26, bf16[128,16384]{1,0:T(8,128)(2,1)} %bitcast.27, ...), custom_call_target="tpu_custom_call" | custom-call | tf_op jit(solution)/shard_map/pallas_call | solution.py:506
  214.7 1.7 copy.26
  216.4 1.7 copy.27
  218.0 0.0 copy-start.1
  218.0 0.0 copy-start
  218.0 0.0 copy-start.3
  218.0 0.0 copy-start.2
  218.0 4.6 %copy.28 = bf16[1,128,16384]{2,1,0:T(8,128)(2,1)} copy(bf16[1,128,16384]{2,1,0:T(8,128)(2,1)} %bitcast.31) | data formatting | bytes 8388608
  222.7 0.0 copy-done.1
  222.7 0.7 copy.29
  223.3 0.0 copy-done
  223.3 0.7 copy.30
  224.0 0.0 copy-done.3
  224.0 0.6 copy.31
  224.6 0.0 copy-done.2
  224.6 0.6 copy.32
Async XLA Ops:
  218.0 4.6 %copy-start.1 = (f32[16,2048]{1,0:T(8,128)S(1)}, f32[16,2048]{1,0:T(8,128)}, u32[]{:S(2)}) copy-start(f32[16,2048]{1,0:T(8,128)} %get-tuple-element.17) | copy-start | bytes 393220
  218.0 5.3 %copy-start = (f32[16,2048]{1,0:T(8,128)S(1)}, f32[16,2048]{1,0:T(8,128)}, u32[]{:S(2)}) copy-start(f32[16,2048]{1,0:T(8,128)} %get-tuple-element.18) | copy-start | bytes 393220
  218.0 5.9 %copy-start.3 = (f32[16,128]{1,0:T(8,128)S(1)}, f32[16,128]{1,0:T(8,128)}, u32[]{:S(2)}) copy-start(f32[16,128]{1,0:T(8,128)} %get-tuple-element.19) | copy-start | bytes 24580
  218.0 6.5 %copy-start.2 = (f32[16,128]{1,0:T(8,128)S(1)}, f32[16,128]{1,0:T(8,128)}, u32[]{:S(2)}) copy-start(f32[16,128]{1,0:T(8,128)} %get-tuple-element.20) | copy-start | bytes 24580

commit v3 on v2

--- a/solution.py
+++ b/solution.py
@@ -14,8 +14,8 @@
 BF16 = jnp.bfloat16
 MESH = pl.DeviceIdType.MESH
 
-UPK, UPV, DNK, DNV, COT, XAT, XIN, INV, RET, BRA, GRD, MID, PAR, TOT = range(14)
-KINDS = 14
+UPK, UPV, DNK, DNV, COTK, COTV, XAT, XIN, INV, RET, BRA, GRD, GRY, MID, PAR, TOT = range(16)
+KINDS = 16
 
 
 PROFILE = False
@@ -32,10 +32,11 @@
 def kernel(
     S, Y, Z,
     arr, kept, ret, gain, wk, wv, dkt, dvt, uk, uv, ck, cv,
-    keys, vals, igrad, gkt, gvt, guk, guv,
-    wb, cf, xin, xat, kb, back, bro, bri, yo, yi, yco, yci, yt, ys, yr, dnf, gdo, gdi, upf,
+    keys_h, vals_h, igrad, gkt_h, gvt_h, guk_h, guv_h,
+    keys, vals, gkt, gvt, guk, guv,
+    wb, cf, xin, xat, kb, back, bro, bri, yo, yi, yco, yci, yt, ys, yr, dnf, gdo, gdi, gds, gdr, upf,
     inv_o, inv_i, mid_o, mid_i, inv_b,
-    ss, rs, css, crs, yss, yrs, ls, ols,
+    ss, rs, yss, yrs, ls, ols,
 ):
     sec = lax.axis_index("section")
     t = lax.axis_index("tensor")
@@ -79,25 +80,60 @@
             send(uv, upf.at[pl.ds(RK, RK), vblk(r)], UPV, i, dev),
         )
 
-    def downs(i, r):
-        dev = (sec, to(i))
-        return (
-            send(dkt, dnf.at[pl.ds(0, RK), blk(r, DS)], DNK, i, dev),
-            send(dvt, dnf.at[pl.ds(RK, RK), blk(r, DS)], DNV, i, dev),
-        )
-
-    def cot_part(v, i, q, r, own):
-        at, to_at = (blk(q, H), blk(r, H)) if v == 0 else (vblk(q), vblk(r))
+    def place(kind, v, b):
+        if kind == COTK:
+            return cf.at[:, blk(b, H) if v == 0 else vblk(b)]
+        return dnf.at[pl.ds(v * RK, RK), blk(b, DS)]
+
+    def spread_part(kind, v, i, q, r, own=False):
         dy, dz = i // Z, i % Z
         if dz == 2:
             dev = (sec, to(1 if v == 0 else Z - 1))
         else:
             dev = (sec, to(dz if dz else dy * Z))
-        src = (ck, cv)[v] if own else cf.at[:, at]
-        return remote(src, cf.at[:, to_at], css.at[v, i], crs.at[v, i], dev)
-
-    def cots(i, q, r, own=False):
-        return [cot_part(v, i, q, r, own) for v in range(2)]
+        src = ((ck, cv) if kind == COTK else (dkt, dvt))[v] if own else place(kind, v, q)
+        return send(src, place(kind, v, r), kind + v, i, dev)
+
+    def spread(kind, i, q, r, own=False):
+        return [spread_part(kind, v, i, q, r, own) for v in range(2)]
+
+    def spread_own(kind):
+        for dy in range(1, Y):
+            for c in spread(kind, dy * Z, t, t, True):
+                c.start()
+        for i in (1, Z - 1):
+            for c in spread(kind, i, t, t, True):
+                c.start()
+
+    def spread_wait(kind, i):
+        for c in spread(kind, i, t, frm(i)):
+            c.wait_recv()
+
+    def spread_halves(kind, dy):
+        for v in range(2):
+            q = frm(dy * Z + (1 if v == 0 else Z - 1))
+            spread_part(kind, v, dy * Z + 2, q, q).start()
+
+    def spread_on(kind):
+        for dy in range(1, Y):
+            spread_wait(kind, dy * Z)
+            q = frm(dy * Z)
+            for dz in (1, Z - 1):
+                for c in spread(kind, dy * Z + dz, q, q):
+                    c.start()
+        for i in (1, Z - 1):
+            spread_wait(kind, i)
+        spread_halves(kind, 0)
+
+    def spread_on_2(kind):
+        for dy in range(1, Y):
+            for dz in (1, Z - 1):
+                spread_wait(kind, dy * Z + dz)
+            spread_halves(kind, dy)
+
+    def spread_end(kind):
+        for dy in range(Y):
+            spread_wait(kind, dy * Z + 2)
 
     def xfirst(i, r):
         dy, dz = i // Z, i % Z
@@ -118,8 +154,12 @@
     def bras(i):
         return send(bro.at[to(i)], bri.at[i], BRA, i, (sec, to(i)))
 
-    def grds(i):
-        return send(gdo.at[to(i)], gdi.at[i], GRD, i, (sec, to(i)))
+    def grds(dz, w):
+        zz = lax.rem(z + dz, Z)
+        return send(gdo.at[w * Z + zz], gdi.at[dz * Y + w], GRD, dz * Y + w, (sec, to(dz)))
+
+    def grys(dy):
+        return send(gds.at[dy], gdr.at[dy], GRY, dy, (sec, to(dy * Z)))
 
     def mids(i):
         return send(mid_o, mid_i.at[i], MID, i, (sec, to(i)))
@@ -173,18 +213,20 @@
     upf[pl.ds(0, RK), pl.ds(KV, KV)] = jnp.zeros((RK, KV), BF16)
     upf[pl.ds(RK, RK), pl.ds(0, KV)] = jnp.zeros((RK, KV), BF16)
 
+    outs = [
+        pltpu.make_async_copy(a, b, ols.at[T + n])
+        for n, (a, b) in enumerate([(keys, keys_h), (vals, vals_h), (gkt, gkt_h), (gvt, gvt_h), (guk, guk_h), (guv, guv_h)])
+    ]
+
     with scope("barrier"):
         pl.semaphore_wait(bar, 3 * T - 1)
 
     for i in range(1, T):
         for c in ups(i, t):
             c.start()
-    for dy in range(1, Y):
-        for c in cots(dy * Z, t, t, True):
-            c.start()
-    for i in (1, Z - 1):
-        for c in cots(i, t, t, True):
-            c.start()
+    spread_own(COTK)
+    spread_own(DNK)
+
     with scope("stats_a"):
         for c in arrs:
             c.wait()
@@ -199,25 +241,8 @@
         for i in range(T):
             invs(i).start()
 
-    def cot_wait(i):
-        for c in cots(i, t, frm(i)):
-            c.wait_recv()
-
-    def cot_halves(dy):
-        for v in range(2):
-            q = frm(dy * Z + (1 if v == 0 else Z - 1))
-            cot_part(v, dy * Z + 2, q, q, False).start()
-
     with scope("cot_on"):
-        for dy in range(1, Y):
-            cot_wait(dy * Z)
-            q = frm(dy * Z)
-            for dz in (1, Z - 1):
-                for c in cots(dy * Z + dz, q, q):
-                    c.start()
-        for i in (1, Z - 1):
-            cot_wait(i)
-        cot_halves(0)
+        spread_on(COTK)
         for i in range(T):
             xfirst(i, t).start()
 
@@ -255,18 +280,12 @@
                 xon(i, 0, frm(dy * Z)).start()
 
     with scope("wait_cot"):
-        for dy in range(1, Y):
-            for dz in (1, Z - 1):
-                cot_wait(dy * Z + dz)
-            cot_halves(dy)
-        for dy in range(Y):
-            cot_wait(dy * Z + 2)
-    for i in range(1, T):
-        for c in downs(i, t):
-            c.start()
-    for dy in range(Y):
-        x_on(dy)
-    rets().start()
+        spread_on(DNK)
+        spread_on_2(COTK)
+        spread_end(COTK)
+    with scope("wait_down"):
+        spread_on_2(DNK)
+    x_on(0)
     NT = 512
 
     def branch(p, store):
@@ -287,7 +306,12 @@
         bri[0, :, pl.ds(n * NT, NT)] = v
 
     with scope("branch"):
-        lax.fori_loop(1, T, branch_to, 0)
+        lax.fori_loop(Z, T, branch_to, 0)
+    for dy in range(1, Y):
+        x_on(dy)
+    rets().start()
+    with scope("branch"):
+        lax.fori_loop(1, Z, branch_to, 0)
         branch(t, store_own)
 
     def forward_block(i, r):
@@ -304,12 +328,37 @@
         forward_block(i, frm(i))
         return 0
 
+    def kept_normed(p):
+        cols = blk(p, DS)
+        return (kb[:, cols].astype(F32) * inv_b[:, 0:1] * gain[:, cols].astype(F32)).astype(BF16)
+
+    with scope("kept"):
+        adapt = (SCALE * dot(upf[...], cf[blk(t, R), :], 1, 1)).astype(BF16)
+
+        def grad_block(p, _):
+            gdo[p] = dot(adapt, kept_normed(p), 1, 0).astype(BF16)
+            return 0
+
+        lax.fori_loop(0, T, grad_block, 0)
+    with scope("middle"):
+        spread_end(DNK)
+
+        def middle_block(p, mid):
+            return mid + dot(dnf[:, blk(p, DS)], kept_normed(p), 1, 1)
+
+        mid_o[...] = lax.fori_loop(0, T, middle_block, jnp.zeros((2 * RK, R), F32)).astype(BF16)
+        for i in range(1, T):
+            mids(i).start()
+
     with scope("wait_x"):
         for i in range(T):
             if i % Z:
                 send(xat.at[0], xin.at[blk(frm(i), R), :], XIN, i, (sec, to(i % Z))).wait_recv()
-    for i in range(1, T):
+    for i in range(Z, T):
         bras(i).start()
+    for dz in range(1, Z):
+        for w in range(Y):
+            grds(dz, w).start()
 
     with scope("forward"):
         for g in range(Y):
@@ -319,29 +368,6 @@
             for k in range(4):
                 for c in parts(g, k):
                     c.start()
-
-    with scope("kept"):
-        for i in range(1, T):
-            for c in downs(i, frm(i)):
-                c.wait_recv()
-        adapt = (SCALE * dot(upf[...], cf[blk(t, R), :], 1, 1)).astype(BF16)
-
-        def kept_block(i, mid):
-            p = to(i)
-            cols = blk(p, DS)
-            normed = (kb[:, cols].astype(F32) * inv_b[:, 0:1] * gain[:, cols].astype(F32)).astype(BF16)
-            gdo[p] = dot(adapt, normed, 1, 0).astype(BF16)
-
-            @pl.when(i > 0)
-            def _():
-                grds(i).start()
-
-            return mid + dot(dnf[:, cols], normed, 1, 1)
-
-        mid = lax.fori_loop(0, T, kept_block, jnp.zeros((2 * RK, R), F32))
-        mid_o[...] = mid.astype(BF16)
-        for i in range(1, T):
-            mids(i).start()
 
     def rows_of(g, b, j):
         return blk(g * Z + lax.rem(z + 2 * Z - j - b, Z), R)
@@ -372,34 +398,26 @@
             for v in range(2):
                 pairs(g, v, row).start()
 
-    with scope("wait_branch"):
-        for i in range(1, T):
-            bras(i).wait_recv()
-
-    with scope("inner"):
-
-        def inner_block(i, acc):
-            cols = blk(frm(i), DS)
-            scaled = gain[:, cols].astype(F32) * bri[i].astype(F32)
-            return acc + jnp.sum(kb[:, cols].astype(F32) * scaled, axis=-1, keepdims=True)
-
-        inner = lax.fori_loop(0, T, inner_block, jnp.zeros((R, 1), F32)) / D
-    with scope("wait_ret"):
-        rets().wait_recv()
-    with scope("final"):
-        inverse = inv_b[:, 0:1]
-        factor = inverse * inverse * inverse * inner
-
-        def final_block(i, _):
-            cols = blk(frm(i), DS)
-            scaled = gain[:, cols].astype(F32) * bri[i].astype(F32)
-            back[:, cols] = (
-                back[:, cols].astype(F32) + inverse * scaled - kb[:, cols].astype(F32) * factor
-            ).astype(BF16)
-            pltpu.make_async_copy(back.at[:, cols], igrad.at[:, cols], ols.at[i]).start()
-            return 0
-
-        lax.fori_loop(0, T, final_block, 0)
+    for i in range(1, Z):
+        bras(i).start()
+
+    with scope("grads_z"):
+        for dz in range(1, Z):
+            for w in range(Y):
+                grds(dz, w).wait_recv()
+
+        def grad_sum(w):
+            acc = gdo[w * Z + z].astype(F32)
+            for dz in range(1, Z):
+                acc = acc + gdi[dz * Y + w].astype(F32)
+            return acc
+
+        for dy in range(1, Y):
+            gds[dy] = grad_sum(lax.rem(y + dy, Y)).astype(BF16)
+            grys(dy).start()
+        own_grad = grad_sum(y)
+        gkt[...] = own_grad[0:RK]
+        gvt[...] = own_grad[RK : 2 * RK]
 
     for g in range(Y):
         with scope("wait_parts"):
@@ -431,14 +449,12 @@
                 tots(g, dy, row).start()
 
     with scope("grads"):
+        for dy in range(1, Y):
+            grys(dy).wait_recv()
+            gkt[...] = gkt[...] + gdr[dy, 0:RK].astype(F32)
+            gvt[...] = gvt[...] + gdr[dy, RK : 2 * RK].astype(F32)
         for i in range(1, T):
-            grds(i).wait_recv()
             mids(i).wait_recv()
-        g = gdo[t].astype(F32)
-        for i in range(1, T):
-            g = g + gdi[i].astype(F32)
-        gkt[...] = g[0:RK]
-        gvt[...] = g[RK : 2 * RK]
 
         def up_grad(i, acc):
             m = mid_i[i]
@@ -451,6 +467,8 @@
         k, v = lax.fori_loop(0, T, up_grad, (jnp.zeros((RK, H), F32), jnp.zeros((RK, H), F32)))
         guk[...] = SCALE * k
         guv[...] = SCALE * v
+        for c in outs[2:]:
+            c.start()
 
     with scope("wait_tot"):
         for g in range(Y):
@@ -470,14 +488,47 @@
 
     with scope("total"):
         lax.fori_loop(0, T, total_block, 0)
+        for c in outs[:2]:
+            c.start()
+
+    with scope("inner"):
+
+        def inner_block(i, acc):
+            cols = blk(frm(i), DS)
+            scaled = gain[:, cols].astype(F32) * bri[i].astype(F32)
+            return acc + jnp.sum(kb[:, cols].astype(F32) * scaled, axis=-1, keepdims=True)
+
+        inner = inner_block(0, jnp.zeros((R, 1), F32))
+        for i in (*range(Z, T), *range(1, Z)):
+            bras(i).wait_recv()
+            inner = inner_block(i, inner)
+        inner = inner / D
+    with scope("wait_ret"):
+        rets().wait_recv()
+    with scope("final"):
+        inverse = inv_b[:, 0:1]
+        factor = inverse * inverse * inverse * inner
+
+        def final_block(i, _):
+            cols = blk(frm(i), DS)
+            scaled = gain[:, cols].astype(F32) * bri[i].astype(F32)
+            back[:, cols] = (
+                back[:, cols].astype(F32) + inverse * scaled - kb[:, cols].astype(F32) * factor
+            ).astype(BF16)
+            pltpu.make_async_copy(back.at[:, cols], igrad.at[:, cols], ols.at[i]).start()
+            return 0
+
+        lax.fori_loop(0, T, final_block, 0)
 
     with scope("end"):
         for i in range(1, T):
-            for c in (*ups(i, t), *downs(i, t), bras(i), grds(i), mids(i)):
+            for c in (*ups(i, t), *spread(COTK, i, t, t), *spread(DNK, i, t, t), bras(i), mids(i)):
                 c.wait_send()
-        for i in range(1, T):
-            for c in cots(i, t, t):
-                c.wait_send()
+        for dz in range(1, Z):
+            for w in range(Y):
+                grds(dz, w).wait_send()
+        for dy in range(1, Y):
+            grys(dy).wait_send()
         for g in range(Y):
             for k in range(4):
                 for c in parts(g, k):
@@ -494,6 +545,28 @@
             cols = blk(frm(i), DS)
             pltpu.make_async_copy(back.at[:, cols], igrad.at[:, cols], ols.at[i]).wait()
         rets().wait_send()
+        for c in outs:
+            c.wait()
+
+
+def hand_on(cuts, *refs):
+    n = len(cuts)
+    src, dst, mid, (sem_in, sem_out) = refs[:n], refs[n : 2 * n], refs[2 * n : 3 * n], refs[3 * n :]
+    ins, outs = [], []
+    for a, b, m, cut in zip(src, dst, mid, cuts):
+        rows = a.shape[0] // cut
+        for c in range(cut):
+            at = pl.ds(c * rows, rows)
+            k = len(ins)
+            ins.append(pltpu.make_async_copy(a.at[at], m.at[at], sem_in.at[k]))
+            outs.append(pltpu.make_async_copy(m.at[at], b.at[at], sem_out.at[k]))
+    for c in ins:
+        c.start()
+    for c, d in zip(ins, outs):
+        c.wait()
+        d.start()
+    for d in outs:
+        d.wait()
 
 
 def on_device(S, T, arr, kept, ret, gain, wk, wv, dk, dv, uk, uv, ck, cv):
@@ -515,8 +588,14 @@
             jax.ShapeDtypeStruct((RK, H), F32),
         ),
         in_specs=[any_, any_, any_, vmem] + [any_] * 8,
-        out_specs=(vmem, vmem, any_, vmem, vmem, vmem, vmem),
+        out_specs=(any_,) * 7,
         scratch_shapes=[
+            pltpu.VMEM((R * T, H), BF16),
+            pltpu.VMEM((R * T, H), BF16),
+            pltpu.VMEM((RK, DS), F32),
+            pltpu.VMEM((RK, DS), F32),
+            pltpu.VMEM((RK, H), F32),
+            pltpu.VMEM((RK, H), F32),
             pltpu.VMEM((DS, 2 * KV), BF16),
             pltpu.VMEM((R * T, 2 * KV), BF16),
             pltpu.VMEM((R * T, DS), BF16),
@@ -535,6 +614,8 @@
             pltpu.VMEM((2 * RK, D), BF16),
             pltpu.VMEM((T, 2 * RK, DS), BF16),
             pltpu.VMEM((T, 2 * RK, DS), BF16),
+            pltpu.VMEM((Y, 2 * RK, DS), BF16),
+            pltpu.VMEM((Y, 2 * RK, DS), BF16),
             pltpu.VMEM((2 * RK, 2 * KV), BF16),
             pltpu.VMEM((8, R), F32),
             pltpu.VMEM((T, 8, R), F32),
@@ -543,12 +624,10 @@
             pltpu.VMEM((R, R), F32),
             pltpu.SemaphoreType.DMA((KINDS, T)),
             pltpu.SemaphoreType.DMA((KINDS, T)),
-            pltpu.SemaphoreType.DMA((2, T)),
-            pltpu.SemaphoreType.DMA((2, T)),
             pltpu.SemaphoreType.DMA((4 * Y * Y,)),
             pltpu.SemaphoreType.DMA((4 * Y * Y,)),
             pltpu.SemaphoreType.DMA((9 + T,)),
-            pltpu.SemaphoreType.DMA((T,)),
+            pltpu.SemaphoreType.DMA((T + 6,)),
         ],
         compiler_params=pltpu.CompilerParams(
             collective_id=0, has_side_effects=True, vmem_limit_bytes=62 * 2**20
@@ -556,6 +635,15 @@
     )(
         arr[0], kept[0], ret[0], gain, wk[0], wv[0], dk[0].T, dv[0].T, uk[0], uv[0], ck[0], cv[0]
     )
+    cuts = [1, 1, T, 1, 1, 1, 1]
+    outs = pl.pallas_call(
+        functools.partial(hand_on, cuts),
+        out_shape=[jax.ShapeDtypeStruct(o.shape, o.dtype) for o in outs],
+        in_specs=[any_] * 7,
+        out_specs=[any_] * 7,
+        scratch_shapes=[pltpu.VMEM(o.shape, o.dtype) for o in outs]
+        + [pltpu.SemaphoreType.DMA((sum(cuts),)), pltpu.SemaphoreType.DMA((sum(cuts),))],
+    )(*outs)
     keys, vals, igrad, gkt, gvt, guk, guv = outs
     return keys[None], vals[None], igrad[None], gkt.T[None], gvt.T[None], guk[None], guv[None]
 

time: 225 us -> 207 us (0.920)
  local copies, waits for them, and re-layouts: 10.5 us -> 0 us
  Pallas kernels: 214 us -> 206 us
    pallas_call x1, Pallas kernels: 214 us -> 201 us  [on_device(): pl.pallas_call(functools.partial(kernel, S, Y, Z), out_shape=(jax.ShapeDt...]
    unnamed x15 -> x0, local copies, waits for them, and re-layouts: 10.5 us -> none
    pallas_call x0 -> x1, Pallas kernels: none -> 4.59 us  [on_device(): pl.pallas_call(functools.partial(hand_on, cuts), out_shape=[jax.ShapeDtyp...]
where the time goes in v3:
time: 207 us; the launch traced here: 206 us
  Pallas kernels  206 us (100%)
    pallas_call x1, Pallas kernels, on_device(): pl.pallas_call(functools.partial(kernel, S, Y, Z), out_shape=(jax.ShapeDt...  201 us
    pallas_call x1, Pallas kernels, on_device(): pl.pallas_call(functools.partial(hand_on, cuts), out_shape=[jax.ShapeDtyp...  4.59 us

profile of v3, /device:TPU:1, one launch (start us, length us, event | category | flops | bytes accessed | tf_op | source)
XLA Modules:
  0.0 206.4 jit_solution(12721673412313365684)
XLA Ops:
  0.6 201.0 %shard_map.171 = (bf16[1024,128]{1,0:T(8,128)(2,1)}, bf16[1024,128]{1,0:T(8,128)(2,1)}, bf16[128,16384]{1,0:T(8,128)(2,1)}, f32[16,2048]{1,0:T(8,128)}, f32[16,2...) custom-call(bf16[128,16384]{1,0:T(8,128)(2,1)} %bitcast.26, bf16[128,16384]{1,0:T(8,128)(2,1)} %bitcast.27, ...), custom_call_target="tpu_custom_call" | custom-call | tf_op jit(solution)/shard_map/pallas_call | solution.py:579
  201.6 4.6 %shard_map.172 = (bf16[1024,128]{1,0:T(8,128)(2,1)}, bf16[1024,128]{1,0:T(8,128)(2,1)}, bf16[128,16384]{1,0:T(8,128)(2,1)}, f32[16,2048]{1,0:T(8,128)}, f32[16,2...) custom-call(bf16[1024,128]{1,0:T(8,128)(2,1)} %get-tuple-element.21.refs_0_, ...), custom_call_target="tpu_custom_call" | custom-call | tf_op jit(solution)/shard_map/pallas_call | solution.py:639

commit v4 on v3

--- a/solution.py
+++ b/solution.py
@@ -15,7 +15,17 @@
 MESH = pl.DeviceIdType.MESH
 
 UPK, UPV, DNK, DNV, COTK, COTV, XAT, XIN, INV, RET, BRA, GRD, GRY, MID, PAR, TOT = range(16)
-KINDS = 16
+
+
+def slots(Y, Z):
+    T = Y * Z
+    first = [1, 1, 1, 1, 1, 1, 0, 1, 0, 0, 1, Y, 1, 1, 0, 1]
+    count = [T - 1] * 6 + [T, T - 1, T, 1, T - 1, T - Y, Y - 1, T - 1, 2 * Y, 2 * Y - 1]
+    at, base = 0, []
+    for f, n in zip(first, count):
+        base.append(at - f)
+        at += n
+    return base, at
 
 
 PROFILE = False
@@ -49,6 +59,7 @@
     D = T * DS
     nxt = lax.rem(sec + 1, S)
     prv = lax.rem(sec + S - 1, S)
+    base, _ = slots(Y, Z)
     y = t // Z
     z = lax.rem(t, Z)
 
@@ -71,7 +82,7 @@
         )
 
     def send(src, dst, kind, i, device):
-        return remote(src, dst, ss.at[kind, i], rs.at[kind, i], device)
+        return remote(src, dst, ss.at[base[kind] + i], rs.at[base[kind] + i], device)
 
     def ups(i, r):
         dev = (sec, to(i))
@@ -282,10 +293,10 @@
     with scope("wait_cot"):
         spread_on(DNK)
         spread_on_2(COTK)
-        spread_end(COTK)
+    x_on(0)
     with scope("wait_down"):
         spread_on_2(DNK)
-    x_on(0)
+        spread_end(COTK)
     NT = 512
 
     def branch(p, store):
@@ -328,6 +339,9 @@
         forward_block(i, frm(i))
         return 0
 
+    for i in range(Z, T):
+        bras(i).start()
+
     def kept_normed(p):
         cols = blk(p, DS)
         return (kb[:, cols].astype(F32) * inv_b[:, 0:1] * gain[:, cols].astype(F32)).astype(BF16)
@@ -340,22 +354,10 @@
             return 0
 
         lax.fori_loop(0, T, grad_block, 0)
-    with scope("middle"):
-        spread_end(DNK)
-
-        def middle_block(p, mid):
-            return mid + dot(dnf[:, blk(p, DS)], kept_normed(p), 1, 1)
-
-        mid_o[...] = lax.fori_loop(0, T, middle_block, jnp.zeros((2 * RK, R), F32)).astype(BF16)
-        for i in range(1, T):
-            mids(i).start()
-
     with scope("wait_x"):
         for i in range(T):
             if i % Z:
                 send(xat.at[0], xin.at[blk(frm(i), R), :], XIN, i, (sec, to(i % Z))).wait_recv()
-    for i in range(Z, T):
-        bras(i).start()
     for dz in range(1, Z):
         for w in range(Y):
             grds(dz, w).start()
@@ -368,6 +370,16 @@
             for k in range(4):
                 for c in parts(g, k):
                     c.start()
+
+    with scope("middle"):
+        spread_end(DNK)
+
+        def middle_block(p, mid):
+            return mid + dot(dnf[:, blk(p, DS)], kept_normed(p), 1, 1)
+
+        mid_o[...] = lax.fori_loop(0, T, middle_block, jnp.zeros((2 * RK, R), F32)).astype(BF16)
+        for i in range(1, T):
+            mids(i).start()
 
     def rows_of(g, b, j):
         return blk(g * Z + lax.rem(z + 2 * Z - j - b, Z), R)
@@ -470,6 +482,18 @@
         for c in outs[2:]:
             c.start()
 
+    with scope("inner"):
+
+        def inner_block(i, acc):
+            cols = blk(frm(i), DS)
+            scaled = gain[:, cols].astype(F32) * bri[i].astype(F32)
+            return acc + jnp.sum(kb[:, cols].astype(F32) * scaled, axis=-1, keepdims=True)
+
+        inner = inner_block(0, jnp.zeros((R, 1), F32))
+        for i in range(Z, T):
+            bras(i).wait_recv()
+            inner = inner_block(i, inner)
+
     with scope("wait_tot"):
         for g in range(Y):
             for dy in range(1, Y):
@@ -491,15 +515,8 @@
         for c in outs[:2]:
             c.start()
 
-    with scope("inner"):
-
-        def inner_block(i, acc):
-            cols = blk(frm(i), DS)
-            scaled = gain[:, cols].astype(F32) * bri[i].astype(F32)
-            return acc + jnp.sum(kb[:, cols].astype(F32) * scaled, axis=-1, keepdims=True)
-
-        inner = inner_block(0, jnp.zeros((R, 1), F32))
-        for i in (*range(Z, T), *range(1, Z)):
+    with scope("inner_2"):
+        for i in range(1, Z):
             bras(i).wait_recv()
             inner = inner_block(i, inner)
         inner = inner / D
@@ -622,8 +639,8 @@
             pltpu.VMEM((2 * RK, R), BF16),
             pltpu.VMEM((T, 2 * RK, R), BF16),
             pltpu.VMEM((R, R), F32),
-            pltpu.SemaphoreType.DMA((KINDS, T)),
-            pltpu.SemaphoreType.DMA((KINDS, T)),
+            pltpu.SemaphoreType.DMA((slots(Y, Z)[1],)),
+            pltpu.SemaphoreType.DMA((slots(Y, Z)[1],)),
             pltpu.SemaphoreType.DMA((4 * Y * Y,)),
             pltpu.SemaphoreType.DMA((4 * Y * Y,)),
             pltpu.SemaphoreType.DMA((9 + T,)),

time: 207 us -> 204 us (0.986)
  Pallas kernels: 206 us -> 203 us
    pallas_call x1, Pallas kernels: 201 us -> 199 us  [on_device(): pl.pallas_call(functools.partial(kernel, S, Y, Z), out_shape=(jax.ShapeDt...]
where the time goes in v4:
time: 204 us
  Pallas kernels  203 us (100%)
    pallas_call x1, Pallas kernels, on_device(): pl.pallas_call(functools.partial(kernel, S, Y, Z), out_shape=(jax.ShapeDt...  199 us
    pallas_call x1, Pallas kernels, on_device(): pl.pallas_call(functools.partial(hand_on, cuts), out_shape=[jax.ShapeDtyp...  4.59 us

profile of v4, /device:TPU:1, one launch (start us, length us, event | category | flops | bytes accessed | tf_op | source)
XLA Modules:
  0.0 204.2 jit_solution(10878906566137268569)
XLA Ops:
  0.6 198.8 %shard_map.171 = (bf16[1024,128]{1,0:T(8,128)(2,1)}, bf16[1024,128]{1,0:T(8,128)(2,1)}, bf16[128,16384]{1,0:T(8,128)(2,1)}, f32[16,2048]{1,0:T(8,128)}, f32[16,2...) custom-call(bf16[128,16384]{1,0:T(8,128)(2,1)} %bitcast.26, bf16[128,16384]{1,0:T(8,128)(2,1)} %bitcast.27, ...), custom_call_target="tpu_custom_call" | custom-call | tf_op jit(solution)/shard_map/pallas_call | solution.py:596
  199.5 4.6 %shard_map.172 = (bf16[1024,128]{1,0:T(8,128)(2,1)}, bf16[1024,128]{1,0:T(8,128)(2,1)}, bf16[128,16384]{1,0:T(8,128)(2,1)}, f32[16,2048]{1,0:T(8,128)}, f32[16,2...) custom-call(bf16[1024,128]{1,0:T(8,128)(2,1)} %get-tuple-element.21.refs_0_, ...), custom_call_target="tpu_custom_call" | custom-call | tf_op jit(solution)/shard_map/pallas_call | solution.py:656
